TPU v7x, 32 devices: a whole 2x2x4 slice. The times are simulated.
32 devices in a mesh: rep: 4 (over x, y), dp: 8 (over z, core).
Axes of the slice: x: 2, y: 2, z: 4, core: 2. Of those that a mesh axis runs over, the one named last changes fastest.
Arguments:
- x: bfloat16 [32, 2048, 640], P(('rep', 'dp')), parts along dimension 0
- dy: bfloat16 [32, 2048, 640], P(('rep', 'dp')), parts along dimension 0
- w_gate: bfloat16 [2, 640, 2560], replicated
- w_up: bfloat16 [2, 640, 2560], replicated
- w_down: bfloat16 [2, 2560, 640], replicated
- m_w_gate: float32 [2, 640, 2560], P(None, 'dp')
- m_w_up: float32 [2, 640, 2560], P(None, 'dp')
- m_w_down: float32 [2, 2560, 640], P(None, 'dp')
- v_w_gate: float32 [2, 640, 2560], P(None, 'dp')
- v_w_up: float32 [2, 640, 2560], P(None, 'dp')
- v_w_down: float32 [2, 2560, 640], P(None, 'dp')
Outputs:
- output 1: bfloat16 [8, 640, 2560], P('rep'), parts along dimension 0
- output 2: bfloat16 [8, 640, 2560], P('rep'), parts along dimension 0
- output 3: bfloat16 [8, 2560, 640], P('rep'), parts along dimension 0
- output 4: float32 [8, 640, 2560], P('rep', 'dp'), parts along dimension 0
- output 5: float32 [8, 640, 2560], P('rep', 'dp'), parts along dimension 0
- output 6: float32 [8, 2560, 640], P('rep', 'dp'), parts along dimension 0
- output 7: float32 [8, 640, 2560], P('rep', 'dp'), parts along dimension 0
- output 8: float32 [8, 640, 2560], P('rep', 'dp'), parts along dimension 0
- output 9: float32 [8, 2560, 640], P('rep', 'dp'), parts along dimension 0
There are 4 independent parts. A program takes and returns all parts, laid end to end along the dimension named above; an argument that names none is the same for every part.
All inputs are finite; a program needn't handle non-finite values.
Results may differ from a plain program's by a relative error of at most 0.022.
Values are sent between devices in bfloat16 or wider.
A program may use at most 2 GiB of HBM per device.

v0:
```python
import jax
import jax.numpy as jnp
from jax import lax

NAMES = ("w_gate", "w_up", "w_down")


def matmul(a, w):
    return jnp.dot(a, w, preferred_element_type=jnp.float32).astype(jnp.bfloat16)


def normed(h):
    wide = h.astype(jnp.float32)
    scale = lax.rsqrt(jnp.mean(wide**2, -1, keepdims=True) + 1e-6)
    return (wide * scale).astype(jnp.bfloat16)


def layer(h, w):
    a = normed(h)
    gate = jnp.dot(a, w["w_gate"], preferred_element_type=jnp.float32)
    up = jnp.dot(a, w["w_up"], preferred_element_type=jnp.float32)
    return h + matmul((jax.nn.silu(gate) * up).astype(jnp.bfloat16), w["w_down"])


def adamw(w, m, v, g):
    m = 0.9 * m + 0.1 * g
    v = 0.95 * v + 0.05 * g * g
    step = m * lax.rsqrt(v + 1e-8) + 0.1 * w
    return (w - 0.02 * step).astype(jnp.bfloat16), m, v


def stack(weights, h):
    for number in range(weights["w_gate"].shape[0]):
        h = layer(h, {name: w[number] for name, w in weights.items()})
    return h


def solution(mesh):
    groups = mesh.shape["rep"]

    def step(x, dy, *arrays):
        weights, m, v = (arrays[i : i + 3] for i in (0, 3, 6))
        x, dy = (t.reshape(groups, -1, *t.shape[1:]) for t in (x, dy))

        def of_a_group(x, dy):
            _, back = jax.vjp(lambda w: stack(w, x), dict(zip(NAMES, weights, strict=True)))
            by_weights = back(dy)[0]
            gradients = [by_weights[name].astype(jnp.float32) for name in NAMES]
            new = [adamw(w.astype(jnp.float32), m, v, g) for w, m, v, g in zip(weights, m, v, gradients, strict=True)]
            return tuple(one[which] for which in range(3) for one in new)

        return tuple(t.reshape(-1, *t.shape[2:]) for t in jax.vmap(of_a_group)(x, dy))

    return step
```

profile of v0, /device:TPU:0, one launch (start us, length us, event | category | flops | bytes accessed | tf_op | source)
XLA Modules:
  0.0 790.5 jit_solution(14816637856635987483)
XLA Ops:
  7.2 2.5 fusion.47
  9.7 4.4 copy
  14.1 10.3 %fusion.67 = f32[2048,2560]{1,0:T(8,128)S(1)} fusion(bf16[2,640,2560]{2,1,0:T(8,128)(2,1)} %param, bf16[1,2048,640]{2,1,0:T(8,128)(2,1)S(1)} %copy-done.1, f32[2048]{0:T(1024)S(1)} %add_rsqrt_fusion), kind=kOutput, calls=%fused_computation.79 | convolution fusion | flops 6714818560 | bytes 26877952 | tf_op jit(solution)/vmap(jvp())/dot_general | solution.py:20
  24.5 16.3 %fusion.65 = f32[2048,2560]{1,0:T(8,128)} fusion(bf16[2,640,2560]{2,1,0:T(8,128)(2,1)} %param.3, bf16[1,2048,640]{2,1,0:T(8,128)(2,1)S(1)} %copy-done.1, f32[2048]{0:T(1024)S(1)} %add_rsqrt_fusion), kind=kOutput, calls=%fused_computation.77 | convolution fusion | flops 6714818560 | bytes 26877952 | tf_op jit(solution)/vmap(jvp())/dot_general | solution.py:21
  40.8 15.6 %fusion.26 = bf16[2048,2560]{1,0:T(8,128)(2,1)} fusion(f32[2048,2560]{1,0:T(8,128)} %fusion.65, f32[2048,2560]{1,0:T(8,128)S(1)} %fusion.67), kind=kLoop, calls=%fused_computation.37 | loop fusion | flops 31457280 | bytes 52428800
  56.4 11.2 %fusion.51 = (f32[2048]{0:T(1024)S(1)}, bf16[1,1,2048,640]{2,3,1,0:T(8,128)(2,1)S(1)}) fusion(bf16[2048,2560]{1,0:T(8,128)(2,1)} %fusion.26, bf16[2,2560,640]{2,1,0:T(8,128)(2,1)} %param.4, bf16[1,2048,640]{1,2,0:T(8,128)(2,1)S(1)} %copy-done.9), kind=kOutput, calls=%fused_computation.62 | convolution fusion | flops 6717437952 | bytes 19013632 | tf_op jit(solution)/vmap(jvp())/dot_general | solution.py:9
  67.7 0.7 copy-done.16
  68.4 13.6 %fusion.54 = f32[2048,2560]{1,0:T(8,128)} fusion(bf16[2,640,2560]{2,1,0:T(8,128)(2,1)} %param, bf16[1,1,2048,640]{2,3,1,0:T(8,128)(2,1)S(1)} %get-tuple-element.10, f32[2048]{0:T(1024)S(1)} %bitcast.353), kind=kOutput, calls=%fused_computation.66 | convolution fusion | flops 6714818560 | bytes 26877952 | tf_op jit(solution)/vmap(jvp())/dot_general | solution.py:20
  82.0 13.5 %fusion.58 = f32[2048,2560]{1,0:T(8,128)} fusion(bf16[2,640,2560]{2,1,0:T(8,128)(2,1)} %param.3, bf16[1,1,2048,640]{2,3,1,0:T(8,128)(2,1)S(1)} %get-tuple-element.10, f32[2048]{0:T(1024)S(1)} %bitcast.354), kind=kOutput, calls=%fused_computation.70 | convolution fusion | flops 6714818560 | bytes 26877952 | tf_op jit(solution)/vmap(jvp())/dot_general | solution.py:21
  95.5 19.4 %fusion.35 = f32[1,2560,640]{2,1,0:T(8,128)} fusion(f32[2048,2560]{1,0:T(8,128)} %fusion.58, f32[2048,2560]{1,0:T(8,128)} %fusion.54, bf16[1,2048,640]{2,1,0:T(8,128)(2,1)S(1)} %copy-done.8), kind=kOutput, calls=%fused_computation.52 | convolution fusion | flops 6742343680 | bytes 51118080 | tf_op jit(solution)/vmap(transpose(jvp()))/dot_general | solution.py:9
  115.0 3.4 copy.1
  118.4 10.9 %convolution_convert_fusion.1 = bf16[2048,2560]{1,0:T(8,128)(2,1)S(1)} fusion(bf16[2,2560,640]{2,1,0:T(8,128)(2,1)} %param.4, bf16[1,2048,640]{2,1,0:T(8,128)(2,1)} %param.5), kind=kOutput, calls=%fused_computation.36 | convolution fusion | flops 6716129280 | bytes 16384000 | tf_op jit(solution)/vmap(transpose(jvp()))/dot_general | solution.py:9
  129.3 3.9 copy-done.2
  133.2 20.2 %fusion.6 = bf16[2048,2560]{1,0:T(8,128)(2,1)} fusion(f32[2048,2560]{1,0:T(8,128)} %fusion.54, f32[2048,2560]{1,0:T(8,128)} %fusion.58, bf16[2048,2560]{1,0:T(8,128)(2,1)S(1)} %convolution_convert_fusion.1), kind=kLoop, calls=%fused_computation.11 | loop fusion | flops 62914560 | bytes 62914560
  153.4 15.7 %fusion.78 = bf16[2048,640]{0,1:T(8,128)(2,1)} fusion(bf16[2048,2560]{1,0:T(8,128)(2,1)} %copy-done.2, f32[2048,2560]{1,0:T(8,128)} %fusion.54, bf16[2,640,2560]{2,1,0:T(8,128)(2,1)} %param.3), kind=kOutput, calls=%fused_computation.86 | convolution fusion | flops 6743654400 | bytes 37355520 | tf_op jit(solution)/vmap(transpose(jvp()))/dot_general | solution.py:21
  169.1 13.5 %fusion.53 = (f32[2048]{0:T(1024)S(1)}, bf16[2048,640]{0,1:T(8,128)(2,1)S(1)}) fusion(bf16[1,1,2048,640]{2,3,1,0:T(8,128)(2,1)} %copy-done.4, bf16[2048,640]{0,1:T(8,128)(2,1)} %fusion.78, bf16[2048,2560]{1,0:T(8,128)(2,1)} %fusion.6, bf16[2,640,2560]{2,1,0:T(8,128)(2,1)} %param), kind=kOutput, calls=%fused_computation.64 | convolution fusion | flops 6717437952 | bytes 21635072 | tf_op jit(solution)/vmap(transpose(jvp()))/dot_general | solution.py:20
  182.7 1.8 fusion.95
  184.5 1.5 copy-done.7
  186.0 12.9 %convolution_bitcast_fusion = f32[1,2560,640]{2,1,0:T(8,128)} fusion(bf16[2048,2560]{1,0:T(8,128)(2,1)} %fusion.26, bf16[2048,640]{0,1:T(8,128)(2,1)S(1)} %fusion.95), kind=kOutput, calls=%fused_computation.56 | convolution fusion | flops 6710886400 | bytes 19660800 | tf_op jit(solution)/vmap(transpose(jvp()))/dot_general | solution.py:9
  198.9 1.7 copy-done.6
  200.6 11.3 %convolution_bitcast_fusion.1 = f32[1,640,2560]{2,1,0:T(8,128)} fusion(bf16[2048,2560]{1,0:T(8,128)(2,1)} %fusion.6, bf16[1,1,2048,640]{2,3,1,0:T(8,128)(2,1)S(1)} %copy-done.6, f32[2048]{0:T(1024)S(1)} %bitcast.356), kind=kOutput, calls=%fused_computation.57 | convolution fusion | flops 6714818560 | bytes 19668992 | tf_op jit(solution)/vmap(transpose(jvp()))/dot_general | solution.py:20
  212.0 13.8 %convolution_convert_fusion = bf16[2048,2560]{1,0:T(8,128)(2,1)} fusion(bf16[2048,640]{0,1:T(8,128)(2,1)} %copy-done.7, bf16[2,2560,640]{2,1,0:T(8,128)(2,1)} %param.4), kind=kOutput, calls=%fused_computation.35 | convolution fusion | flops 6716129280 | bytes 16384000 | tf_op jit(solution)/vmap(transpose(jvp()))/dot_general | solution.py:9
  225.8 22.4 %fusion.41 = f32[1,640,2560]{2,1,0:T(8,128)} fusion(f32[2048,2560]{1,0:T(8,128)} %copy-done, f32[2048,2560]{1,0:T(8,128)} %fusion.65, bf16[2048,2560]{1,0:T(8,128)(2,1)} %convolution_convert_fusion, bf16[1,2048,640]{1,2,0:T(8,128)(2,1)S(1)} %copy-done.10, f32[2048]{0:T(1024)S(1)} %copy-done.19), kind=kOutput, calls=%fused_computation.54 | convolution fusion | flops 6772490240 | bytes 61612032 | tf_op jit(solution)/vmap(transpose(jvp()))/dot_general | solution.py:20
  248.3 15.8 %fusion.38 = f32[1,640,2560]{2,1,0:T(8,128)} fusion(bf16[2048,2560]{1,0:T(8,128)(2,1)} %copy-done.2, f32[2048,2560]{1,0:T(8,128)} %fusion.54, bf16[1,1,2048,640]{2,3,1,0:T(8,128)(2,1)S(1)} %copy-done.6, f32[2048]{0:T(1024)S(1)} %bitcast.357), kind=kOutput, calls=%fused_computation.53 | convolution fusion | flops 6746275840 | bytes 40640512 | tf_op jit(solution)/vmap(transpose(jvp()))/dot_general | solution.py:21
  264.2 1.7 copy-done.11
  265.8 16.0 %fusion.44 = f32[1,640,2560]{2,1,0:T(8,128)} fusion(bf16[2048,2560]{1,0:T(8,128)(2,1)} %convolution_convert_fusion, f32[2048,2560]{1,0:T(8,128)} %copy-done, bf16[1,2048,640]{1,2,0:T(8,128)(2,1)S(1)} %copy-done.11, f32[2048]{0:T(1024)S(1)} %copy-done.19), kind=kOutput, calls=%fused_computation.55 | convolution fusion | flops 6746275840 | bytes 40640512 | tf_op jit(solution)/vmap(transpose(jvp()))/dot_general | solution.py:21
  281.9 0.6 copy-done.20
  282.5 0.6 dynamic-slice
  283.7 1.9 convert_bitcast_fusion.4
  285.7 1.2 convert_bitcast_fusion.3
  286.9 4.1 fusion.136
  291.1 56.5 %reduce-scatter.19.cloned.1.call-done = f32[1,80,2560]{2,1,0:T(8,128)} async-done(((f32[1,640,2560]{2,1,0:T(8,128)}), f32[1,80,2560]{2,1,0:T(8,128)}) %reduce-scatter.19.cloned.1.call-update) | async-done | bytes 819216
  347.6 1.9 convert_bitcast_fusion.8
  349.5 71.7 %reduce-scatter.21.cloned.1.call-done = f32[1,80,2560]{2,1,0:T(8,128)} async-done(((f32[1,640,2560]{2,1,0:T(8,128)}), f32[1,80,2560]{2,1,0:T(8,128)}) %reduce-scatter.21.cloned.1.call-update) | async-done | bytes 819216
  421.2 1.2 convert_bitcast_fusion.7
  422.4 5.3 fusion.138
  427.7 66.5 %reduce-scatter.23.cloned.1.call-done = f32[1,80,2560]{2,1,0:T(8,128)} async-done(((f32[1,640,2560]{2,1,0:T(8,128)}), f32[1,80,2560]{2,1,0:T(8,128)}) %reduce-scatter.23.cloned.1.call-update) | async-done | bytes 819216
  494.2 1.9 convert_bitcast_fusion.6
  496.2 71.7 %reduce-scatter.25.cloned.1.call-done = f32[1,80,2560]{2,1,0:T(8,128)} async-done(((f32[1,640,2560]{2,1,0:T(8,128)}), f32[1,80,2560]{2,1,0:T(8,128)}) %reduce-scatter.25.cloned.1.call-update) | async-done | bytes 819216
  567.8 1.2 convert_bitcast_fusion.5
  569.0 4.1 fusion.137
  573.2 61.3 %all-gather.14.cloned.1.call-done = bf16[1,2,2560,640]{3,2,1,0:T(8,128)(2,1)} async-done(((bf16[1,2,320,640]{3,2,1,0:T(8,128)(2,1)}), bf16[1,2,2560,640]{3,2,1,0:T(8,128)(2,1)}) %all-gather.14.cloned.1.call-update) | async-done | bytes 6553616 | tf_op jit(solution)/reshape | solution.py:52
  634.5 67.4 %all-gather.10.cloned.1.call-done = bf16[1,2,640,2560]{3,2,1,0:T(8,128)(2,1)} async-done(((bf16[1,2,80,2560]{3,2,1,0:T(8,128)(2,1)}), bf16[1,2,640,2560]{3,2,1,0:T(8,128)(2,1)}) %all-gather.10.cloned.1.call-update) | async-done | bytes 6553616 | tf_op jit(solution)/reshape | solution.py:52
  701.8 67.4 %all-gather.12.cloned.1.call-done = bf16[1,2,640,2560]{3,2,1,0:T(8,128)(2,1)} async-done(((bf16[1,2,80,2560]{3,2,1,0:T(8,128)(2,1)}), bf16[1,2,640,2560]{3,2,1,0:T(8,128)(2,1)}) %all-gather.12.cloned.1.call-update) | async-done | bytes 6553616 | tf_op jit(solution)/reshape | solution.py:52
  769.2 6.8 copy.5
  776.0 3.3 copy.6
  779.3 1.4 slice-done.1
  780.7 2.8 copy.7
  (64 shorter events, 0.7 us)
Async XLA Ops:
  7.2 6.9 copy-start.1
  7.2 276.5 %reduce-scatter.27.cloned.1.call-start = ((), (), s32[]{:S(2)}) async-start(), calls=%async_computation.13 | async-start | bytes 7372800
  14.1 10.4 %copy-start.18 = (f32[2048]{0:T(1024)}, f32[2048]{0:T(1024)S(1)}, u32[]{:S(2)}) copy-start(f32[2048]{0:T(1024)S(1)} %add_rsqrt_fusion) | copy-start | bytes 24580
  24.5 16.3 %copy-start = (f32[2048,2560]{1,0:T(8,128)}, f32[2048,2560]{1,0:T(8,128)S(1)}, u32[]{:S(2)}) copy-start(f32[2048,2560]{1,0:T(8,128)S(1)} %fusion.67) | copy-start | bytes 62914564
  40.8 15.6 %copy-start.9 = (bf16[1,2048,640]{1,2,0:T(8,128)(2,1)S(1)}, bf16[1,2048,640]{1,2,0:T(8,128)(2,1)}, u32[]{:S(2)}) copy-start(bf16[1,2048,640]{1,2,0:T(8,128)(2,1)} %copy) | copy-start | bytes 7864324
  67.6 14.3 %copy-start.4 = (bf16[1,1,2048,640]{2,3,1,0:T(8,128)(2,1)}, bf16[1,1,2048,640]{2,3,1,0:T(8,128)(2,1)S(1)}, u32[]{:S(2)}) copy-start(bf16[1,1,2048,640]{2,3,1,0:T(8,128)(2,1)S(1)} %get-tuple-element.10) | copy-start | bytes 7864324
  67.7 0.7 copy-start.16
  82.0 13.5 %copy-start.8 = (bf16[1,2048,640]{2,1,0:T(8,128)(2,1)S(1)}, bf16[1,2048,640]{2,1,0:T(8,128)(2,1)}, u32[]{:S(2)}) copy-start(bf16[1,2048,640]{2,1,0:T(8,128)(2,1)} %param.5) | copy-start | bytes 7864324
  114.9 170.7 %reduce-scatter.29.cloned.1.call-start = ((), (), s32[]{:S(2)}) async-start(), calls=%async_computation.14 | async-start | bytes 7372800
  129.3 3.9 copy-start.2
  169.1 13.5 %copy-start.17 = (f32[2048]{0:T(1024)S(1)}, f32[2048]{0:T(1024)}, u32[]{:S(2)}) copy-start(f32[2048]{0:T(1024)} %copy-done.16) | copy-start | bytes 24580
  169.1 13.5 %copy-start.5 = (bf16[1,1,2048,640]{2,3,1,0:T(8,128)(2,1)S(1)}, bf16[1,1,2048,640]{2,3,1,0:T(8,128)(2,1)}, u32[]{:S(2)}) copy-start(bf16[1,1,2048,640]{2,3,1,0:T(8,128)(2,1)} %copy-done.4) | copy-start | bytes 7864324
  184.5 1.5 copy-start.7
  198.9 1.7 copy-start.6
  198.9 148.7 %reduce-scatter.19.cloned.1.call-start = ((), (), s32[]{:S(2)}) async-start(), calls=%async_computation.9 | async-start | bytes 7372800
  211.9 13.8 %copy-start.19 = (f32[2048]{0:T(1024)S(1)}, f32[2048]{0:T(1024)}, u32[]{:S(2)}) copy-start(f32[2048]{0:T(1024)} %copy-done.18) | copy-start | bytes 24580
  212.0 209.2 %reduce-scatter.21.cloned.1.call-start = ((), (), s32[]{:S(2)}) async-start(), calls=%async_computation.10 | async-start | bytes 7372800
  212.0 13.8 %copy-start.10 = (bf16[1,2048,640]{1,2,0:T(8,128)(2,1)S(1)}, bf16[1,2048,640]{1,2,0:T(8,128)(2,1)}, u32[]{:S(2)}) copy-start(bf16[1,2048,640]{1,2,0:T(8,128)(2,1)} %copy) | copy-start | bytes 7864324
  248.2 246.0 %reduce-scatter.23.cloned.1.call-start = ((), (), s32[]{:S(2)}) async-start(), calls=%async_computation.11 | async-start | bytes 7372800
  264.1 1.7 copy-start.11
  264.1 303.7 %reduce-scatter.25.cloned.1.call-start = ((), (), s32[]{:S(2)}) async-start(), calls=%async_computation.12 | async-start | bytes 7372800
  281.8 0.7 copy-start.20
  281.8 5.1 copy-start.12
  281.8 5.1 copy-start.13
  281.8 352.6 %all-gather.14.cloned.1.call-start = ((), (), s32[]{:S(2)}) async-start(), calls=%async_computation.8 | async-start | bytes 7372800 | tf_op jit(solution)/reshape | solution.py:52
  291.1 410.8 %all-gather.10.cloned.1.call-start = ((), (), s32[]{:S(2)}) async-start(), calls=%async_computation.6 | async-start | bytes 7372800 | tf_op jit(solution)/reshape | solution.py:52
  422.4 146.6 %copy-start.14 = (f32[2,80,2560]{2,1,0:T(8,128)S(1)}, f32[2,80,2560]{2,1,0:T(8,128)}, u32[]{:S(2)}) copy-start(f32[2,80,2560]{2,1,0:T(8,128)} %param.8) | copy-start | bytes 4915204
  422.4 146.6 %copy-start.15 = (f32[2,80,2560]{2,1,0:T(8,128)S(1)}, f32[2,80,2560]{2,1,0:T(8,128)}, u32[]{:S(2)}) copy-start(f32[2,80,2560]{2,1,0:T(8,128)} %param.7) | copy-start | bytes 4915204
  427.7 341.5 %all-gather.12.cloned.1.call-start = ((), (), s32[]{:S(2)}) async-start(), calls=%async_computation.7 | async-start | bytes 7372800 | tf_op jit(solution)/reshape | solution.py:52
  769.2 6.8 copy-start.3
  769.2 10.1 %slice-start = ((s8[6553600]{0:T(1024)(128)(4,1)}), s8[4194304]{0:T(1024)(128)(4,1)S(1)}, s32[]{:S(2)}) async-start(s8[6553600]{0:T(1024)(128)(4,1)} %bitcast.345), calls=%async_computation.15 | async-start | bytes 8388608
  776.0 4.7 slice-start.1
Sparse Core Ops, SparseCore 0:
  115.1 74.7 reduce-scatter.26
  199.0 74.7 reduce-scatter.28
  276.7 70.8 reduce-scatter.18
  350.3 70.8 reduce-scatter.20
  423.4 70.8 reduce-scatter.22
  497.0 70.8 reduce-scatter.24
  569.4 65.0 all-gather.13
  636.7 65.1 all-gather.9
  704.0 65.1 all-gather.11
where the time goes:
time: 799 us; the launch traced here: 790 us
  waiting for transfers between devices  462 us (58%)
  matrix products  217 us (27%)
  other arithmetic  63 us (8%)
  local copies, waits for them, and re-layouts  32.7 us (4%)
  between operations  15.2 us (2%)
    unnamed x15, waiting for transfers between devices  266 us
    reshape x3, waiting for transfers between devices, step(): t.reshape(-1, *t.shape[2:])  196 us
    dot_general x5, matrix products, layer(): up = jnp.dot(a, w['w_up'], preferred_element_type=jnp.float32)  77.3 us
    dot_general x5, matrix products, layer(): gate = jnp.dot(a, w['w_gate'], preferred_element_type=jnp.float32)  71.2 us
    dot_general x5, matrix products, matmul(): jnp.dot(a, w, preferred_element_type=jnp.float32).astype(jnp.bfloat16)  68.2 us
    unnamed x4, other arithmetic  37.6 us
    unnamed x51, local copies, waits for them, and re-layouts  32.1 us
  transfers between devices with their start and end apart: 9, of which 7 were waited for; matrix products, arithmetic and copies ran while one was open for 23% of the time, Pallas kernels for 0%

commit v1 on v0

v1 whole, which is shorter than its diff:
```python
import jax
import jax.numpy as jnp
from jax import lax
from jax.sharding import PartitionSpec as P

NAMES = ("w_gate", "w_up", "w_down")


def normed(h):
    wide = h.astype(jnp.float32)
    scale = lax.rsqrt(jnp.mean(wide**2, -1, keepdims=True) + 1e-6)
    return (wide * scale).astype(jnp.bfloat16)


def matmul(a, w):
    return jnp.dot(a, w, preferred_element_type=jnp.float32).astype(jnp.bfloat16)


def layer(h, w):
    a = normed(h)
    gate = jnp.dot(a, w["w_gate"], preferred_element_type=jnp.float32)
    up = jnp.dot(a, w["w_up"], preferred_element_type=jnp.float32)
    return h + matmul((jax.nn.silu(gate) * up).astype(jnp.bfloat16), w["w_down"])


def adamw(w, m, v, g):
    m = 0.9 * m + 0.1 * g
    v = 0.95 * v + 0.05 * g * g
    step = m * lax.rsqrt(v + 1e-8) + 0.1 * w
    return (w - 0.02 * step).astype(jnp.bfloat16), m, v


def solution(mesh):
    n = mesh.shape["dp"]

    def step(x, dy, *arrays):
        weights, m, v = (arrays[i : i + 3] for i in (0, 3, 6))
        h, by_y = x[0], dy[0]
        layers = weights[0].shape[0]
        me = lax.axis_index("dp")
        backs = []
        for number in range(layers):
            h, back = jax.vjp(layer, h, {name: w[number] for name, w in zip(NAMES, weights)})
            backs.append(back)
        new = {}
        for number in reversed(range(layers)):
            by_y, by_w = backs[number](by_y)
            for k in (2, 0, 1):
                g = lax.psum_scatter(by_w[NAMES[k]], "dp", scatter_dimension=0, tiled=True)
                g = g.astype(jnp.float32)
                rows = g.shape[0]
                w = lax.dynamic_slice_in_dim(weights[k][number], me * rows, rows, 0)
                one, m1, v1 = adamw(w.astype(jnp.float32), m[k][number], v[k][number], g)
                new[k, number] = (lax.all_gather(one, "dp", axis=0, tiled=True), m1, v1)
        return tuple(jnp.stack([new[k, number][which] for number in range(layers)]) for which in range(3) for k in range(3))

    whole = P(None, None, None)
    rows = P(None, "dp", None)
    seq = P(("rep", "dp"), None, None)
    return jax.shard_map(
        step,
        mesh=mesh,
        in_specs=(seq, seq) + (whole,) * 3 + (rows,) * 6,
        out_specs=(P("rep", None, None),) * 3 + (P("rep", "dp", None),) * 6,
        check_vma=False,
    )
```

time: 799 us -> 663 us (0.83)
  waiting for transfers between devices: 462 us -> 324 us
  matrix products: 217 us -> 246 us
  other arithmetic: 63 us -> 45.9 us
  local copies, waits for them, and re-layouts: 32.7 us -> 23 us
    unnamed x15 -> x12, waiting for transfers between devices: 266 us -> 1.9 us
    all_gather x0 -> x6, waiting for transfers between devices: none -> 212 us  [step(): new[k, number] = (lax.all_gather(one, 'dp', axis=0, tiled=True), m1, v1)]
    reshape x3 -> x0, waiting for transfers between devices: 196 us -> none  [step(): t.reshape(-1, *t.shape[2:])]
    reduce_scatter x0 -> x6, waiting for transfers between devices: none -> 110 us  [step(): g = lax.psum_scatter(by_w[NAMES[k]], 'dp', scatter_dimension=0, tiled=True)]
    unnamed x4 -> x1, other arithmetic: 37.6 us -> 0.01 us
    another operation x0 -> x6, other arithmetic: none -> 27.1 us  [step(): jnp.stack([new[k, number][which] for number in range(layers)])]
    unnamed x51 -> x44, local copies, waits for them, and re-layouts: 32.1 us -> 7.58 us
    dot_general x5, matrix products: 71.2 us -> 92.9 us  [layer(): gate = jnp.dot(a, w['w_gate'], preferred_element_type=jnp.float32)]
  transfers between devices with their start and end apart: 9 -> 12, of which waited for: 7 -> 9; matrix products, arithmetic and copies ran while one was open for 23% -> 27% of each run, Pallas kernels for 0% -> 0%
where the time goes in v1:
time: 663 us; the launch traced here: 655 us
  waiting for transfers between devices  324 us (49%)
  matrix products  246 us (37%)
  other arithmetic  45.9 us (7%)
  local copies, waits for them, and re-layouts  23 us (3%)
  between operations  14.9 us (2%)
    all_gather x6, waiting for transfers between devices, step(): new[k, number] = (lax.all_gather(one, 'dp', axis=0, tiled=True), m1, v1)  212 us
    reduce_scatter x6, waiting for transfers between devices, step(): g = lax.psum_scatter(by_w[NAMES[k]], 'dp', scatter_dimension=0, tiled=True)  110 us
    dot_general x5, matrix products, layer(): gate = jnp.dot(a, w['w_gate'], preferred_element_type=jnp.float32)  92.9 us
    dot_general x5, matrix products, layer(): up = jnp.dot(a, w['w_up'], preferred_element_type=jnp.float32)  86.5 us
    dot_general x5, matrix products, matmul(): jnp.dot(a, w, preferred_element_type=jnp.float32).astype(jnp.bfloat16)  66.9 us
    another operation x6, other arithmetic, step(): jnp.stack([new[k, number][which] for number in range(layers)])  27.1 us
    convert_element_type x3, other arithmetic, adamw(): return ((w - 0.02 * step).astype(jnp.bfloat16), m, v)  14 us
  transfers between devices with their start and end apart: 12, of which 9 were waited for; matrix products, arithmetic and copies ran while one was open for 27% of the time, Pallas kernels for 0%

profile of v1, /device:TPU:0, one launch (start us, length us, event | category | flops | bytes accessed | tf_op | source)
XLA Modules:
  0.0 654.6 jit_solution(12265494931938307583)
XLA Ops:
  7.2 3.0 copy.20
  10.2 0.6 fusion.15
  10.8 15.3 %fusion.42 = f32[2048,2560]{1,0:T(8,128)} fusion(bf16[1,2048,640]{2,1,0:T(8,128)(2,1)} %param.11, f32[2048]{0:T(1024)S(1)} %add_rsqrt_fusion, bf16[2,640,2560]{2,1,0:T(8,128)(2,1)} %param.13), kind=kOutput, calls=%fused_computation.63 | convolution fusion | flops 6714818560 | bytes 26877952 | tf_op jit(solution)/shard_map/jvp()/dot_general | solution.py:21
  26.1 23.5 %multiply_convert_fusion.1 = (bf16[2048,2560]{1,0:T(8,128)(2,1)}, f32[2048,2560]{1,0:T(8,128)}) fusion(f32[2048,2560]{1,0:T(8,128)} %fusion.42, bf16[2,640,2560]{2,1,0:T(8,128)(2,1)} %param.14, bf16[1,2048,640]{2,1,0:T(8,128)(2,1)} %param.11, f32[2048]{0:T(1024)S(1)} %add_rsqrt_fusion), kind=kOutput, calls=%fused_computation.17 | convolution fusion | flops 6746275840 | bytes 58335232 | tf_op jit(solution)/shard_map/jvp()/dot_general | solution.py:22
  49.6 10.3 %fusion.19 = (f32[2048]{0:T(1024)S(1)}, bf16[2048,640]{0,1:T(8,128)(2,1)S(1)}) fusion(bf16[2048,2560]{1,0:T(8,128)(2,1)} %get-tuple-element.33, bf16[2,2560,640]{2,1,0:T(8,128)(2,1)S(1)} %bitcast.189, bf16[1,2048,640]{1,2,0:T(8,128)(2,1)S(1)} %copy.20), kind=kOutput, calls=%fused_computation.40 | convolution fusion | flops 6717437952 | bytes 19013632 | tf_op jit(solution)/shard_map/jvp()/dot_general | solution.py:16
  60.0 10.8 %convolution_convert_fusion.1 = bf16[2048,2560]{1,0:T(8,128)(2,1)} fusion(bf16[1,2048,640]{2,1,0:T(8,128)(2,1)S(1)} %copy-done.13, bf16[2,2560,640]{2,1,0:T(8,128)(2,1)S(1)} %bitcast.189), kind=kOutput, calls=%fused_computation.23 | convolution fusion | flops 6716129280 | bytes 16384000 | tf_op jit(solution)/shard_map/transpose(jvp())/dot_general | solution.py:16
  70.8 13.4 %fusion.29 = f32[2048,2560]{1,0:T(8,128)} fusion(bf16[2048,640]{0,1:T(8,128)(2,1)S(1)} %get-tuple-element.36, f32[2048]{0:T(1024)S(1)} %fusion.112, bf16[2,640,2560]{2,1,0:T(8,128)(2,1)} %param.14), kind=kOutput, calls=%fused_computation.50 | convolution fusion | flops 6714818560 | bytes 26877952 | tf_op jit(solution)/shard_map/jvp()/dot_general | solution.py:22
  84.3 31.3 %fusion.2 = (bf16[2048,2560]{1,0:T(8,128)(2,1)}, f32[2048,2560]{1,0:T(8,128)}) fusion(f32[2048,2560]{1,0:T(8,128)} %fusion.29, bf16[2048,2560]{1,0:T(8,128)(2,1)} %convolution_convert_fusion.1, bf16[2,640,2560]{2,1,0:T(8,128)(2,1)} %param.13, bf16[2048,640]{0,1:T(8,128)(2,1)} %copy-done.10, f32[2048]{0:T(1024)S(1)} %fusion.112), kind=kOutput, calls=%fused_computation.8 | convolution fusion | flops 6777733120 | bytes 68820992 | tf_op jit(solution)/shard_map/jvp()/dot_general | solution.py:21
  115.6 19.4 %fusion.22 = bf16[2560,640]{1,0:T(8,128)(2,1)} fusion(f32[2048,2560]{1,0:T(8,128)} %fusion.29, bf16[1,2048,640]{2,1,0:T(8,128)(2,1)S(1)} %copy-done.14, f32[2048,2560]{1,0:T(8,128)} %get-tuple-element.38), kind=kOutput, calls=%fused_computation.44 | convolution fusion | flops 6743982080 | bytes 47841280 | tf_op jit(solution)/shard_map/transpose(jvp())/dot_general | solution.py:16
  135.1 3.0 copy.21
  138.1 12.7 %fusion.47 = bf16[2048,640]{0,1:T(8,128)(2,1)} fusion(bf16[2048,2560]{1,0:T(8,128)(2,1)} %get-tuple-element.37, bf16[2,640,2560]{2,1,0:T(8,128)(2,1)} %param.13), kind=kOutput, calls=%fused_computation.66 | convolution fusion | flops 6710886400 | bytes 16384000 | tf_op jit(solution)/shard_map/transpose(jvp())/dot_general | solution.py:21
  150.8 19.1 %fusion.21 = (f32[2048]{0:T(1024)S(1)}, bf16[2048,640]{0,1:T(8,128)(2,1)}) fusion(bf16[2048,640]{0,1:T(8,128)(2,1)} %copy-done.10, bf16[2048,640]{0,1:T(8,128)(2,1)} %fusion.47, bf16[2,640,2560]{2,1,0:T(8,128)(2,1)} %param.14, bf16[2048,2560]{1,0:T(8,128)(2,1)} %convolution_convert_fusion.1, f32[2048,2560]{1,0:T(8,128)} %get-tuple-element.38), kind=kOutput, calls=%fused_computation.42 | convolution fusion | flops 6750205952 | bytes 42606592 | tf_op jit(solution)/shard_map/transpose(jvp())/dot_general | solution.py:22
  169.9 4.3 fusion.54
  174.2 1.5 copy-done.12
  175.7 12.6 %convolution_convert_fusion.2 = bf16[2560,640]{1,0:T(8,128)(2,1)} fusion(bf16[2048,2560]{1,0:T(8,128)(2,1)} %get-tuple-element.33, bf16[2048,640]{0,1:T(8,128)(2,1)S(1)} %fusion.54), kind=kOutput, calls=%fused_computation.47 | convolution fusion | flops 6712524800 | bytes 16384000 | tf_op jit(solution)/shard_map/transpose(jvp())/dot_general | solution.py:16
  188.4 0.0 reduce-scatter.13.cloned.1.call-start
  188.4 15.2 %fusion.23 = bf16[640,2560]{1,0:T(8,128)(2,1)} fusion(bf16[2048,2560]{1,0:T(8,128)(2,1)} %convolution_convert_fusion.1, bf16[2048,640]{0,1:T(8,128)(2,1)S(1)} %copy-done.11, f32[2048]{0:T(1024)S(1)} %fusion.112, f32[2048,2560]{1,0:T(8,128)} %get-tuple-element.38), kind=kOutput, calls=%fused_computation.45 | convolution fusion | flops 6747914240 | bytes 37363712 | tf_op jit(solution)/shard_map/transpose(jvp())/dot_general | solution.py:22
  203.7 0.0 reduce-scatter.11.cloned.1.call-start
  203.8 13.7 %convolution_convert_fusion = bf16[2048,2560]{1,0:T(8,128)(2,1)} fusion(bf16[2048,640]{0,1:T(8,128)(2,1)} %copy-done.12, bf16[2,2560,640]{2,1,0:T(8,128)(2,1)} %param.15), kind=kOutput, calls=%fused_computation.22 | convolution fusion | flops 6716129280 | bytes 16384000 | tf_op jit(solution)/shard_map/transpose(jvp())/dot_general | solution.py:16
  217.4 15.2 %fusion.24 = bf16[640,2560]{1,0:T(8,128)(2,1)} fusion(bf16[2048,2560]{1,0:T(8,128)(2,1)} %convolution_convert_fusion, f32[2048,2560]{1,0:T(8,128)} %fusion.42, bf16[1,2048,640]{1,2,0:T(8,128)(2,1)S(1)} %copy-done.1, f32[2048]{0:T(1024)S(1)} %copy-done.18), kind=kOutput, calls=%fused_computation.46 | convolution fusion | flops 6747914240 | bytes 37363712 | tf_op jit(solution)/shard_map/transpose(jvp())/dot_general | solution.py:22
  232.7 0.0 reduce-scatter.9.cloned.1.call-start
  232.7 11.6 %convolution_convert_fusion.3 = bf16[640,2560]{1,0:T(8,128)(2,1)} fusion(bf16[2048,2560]{1,0:T(8,128)(2,1)} %get-tuple-element.37, bf16[2048,640]{0,1:T(8,128)(2,1)} %copy-done.10, f32[2048]{0:T(1024)S(1)} %fusion.112), kind=kOutput, calls=%fused_computation.48 | convolution fusion | flops 6714818560 | bytes 16392192 | tf_op jit(solution)/shard_map/transpose(jvp())/dot_general | solution.py:21
  244.4 22.0 %fusion.25 = bf16[640,2560]{1,0:T(8,128)(2,1)} fusion(f32[2048,2560]{1,0:T(8,128)} %fusion.42, f32[2048,2560]{1,0:T(8,128)} %get-tuple-element.34, bf16[2048,2560]{1,0:T(8,128)(2,1)} %convolution_convert_fusion, bf16[1,2048,640]{1,2,0:T(8,128)(2,1)S(1)} %copy-done.1, f32[2048]{0:T(1024)S(1)} %copy-done.18), kind=kOutput, calls=%fused_computation.49 | convolution fusion | flops 6774128640 | bytes 58335232 | tf_op jit(solution)/shard_map/transpose(jvp())/dot_general | solution.py:21
  266.4 0.0 all-gather.15.cloned.1.call-start
  266.5 5.2 fusion.127
  271.7 4.6 fusion.90
  276.4 0.7 all-gather.17.cloned.1.call-update
  277.2 5.1 fusion.128
  282.3 35.5 %reduce-scatter.11.cloned.1.call-done = bf16[80,2560]{1,0:T(8,128)(2,1)} async-done(((bf16[640,2560]{1,0:T(8,128)(2,1)}), bf16[80,2560]{1,0:T(8,128)(2,1)}) %reduce-scatter.11.cloned.1.call-update) | async-done | bytes 409616 | tf_op jit(solution)/shard_map/reduce_scatter | solution.py:49
  317.8 4.7 fusion.84
  322.5 0.5 all-gather.13.cloned.1.call-update
  323.1 5.1 fusion.129
  328.2 32.3 %reduce-scatter.9.cloned.1.call-done = bf16[80,2560]{1,0:T(8,128)(2,1)} async-done(((bf16[640,2560]{1,0:T(8,128)(2,1)}), bf16[80,2560]{1,0:T(8,128)(2,1)}) %reduce-scatter.9.cloned.1.call-update) | async-done | bytes 409616 | tf_op jit(solution)/shard_map/reduce_scatter | solution.py:49
  360.5 42.7 %reduce-scatter.7.cloned.1.call-done = bf16[80,2560]{1,0:T(8,128)(2,1)} async-done(((bf16[640,2560]{1,0:T(8,128)(2,1)}), bf16[80,2560]{1,0:T(8,128)(2,1)}) %reduce-scatter.7.cloned.1.call-update) | async-done | bytes 409616 | tf_op jit(solution)/shard_map/reduce_scatter | solution.py:49
  403.1 4.7 fusion.78
  407.9 0.5 all-gather.9.cloned.1.call-update
  408.5 4.1 pad_maximum_fusion.5
  412.6 2.0 pad_maximum_fusion.4
  414.6 1.9 pad_maximum_fusion.3
  416.6 25.9 %all-gather.15.cloned.1.call-done = bf16[2560,640]{1,0:T(8,128)(2,1)} async-done(((bf16[320,640]{1,0:T(8,128)(2,1)}), bf16[2560,640]{1,0:T(8,128)(2,1)}) %all-gather.15.cloned.1.call-update) | async-done | bytes 3276816 | tf_op jit(solution)/shard_map/all_gather | solution.py:54
  442.5 39.8 %all-gather.17.cloned.1.call-done = bf16[2560,640]{1,0:T(8,128)(2,1)} async-done(((bf16[320,640]{1,0:T(8,128)(2,1)}), bf16[2560,640]{1,0:T(8,128)(2,1)}) %all-gather.17.cloned.1.call-update) | async-done | bytes 3276816 | tf_op jit(solution)/shard_map/all_gather | solution.py:54
  482.3 6.4 pad_maximum_fusion.2
  488.7 33.4 %all-gather.11.cloned.1.call-done = bf16[640,2560]{1,0:T(8,128)(2,1)} async-done(((bf16[80,2560]{1,0:T(8,128)(2,1)}), bf16[640,2560]{1,0:T(8,128)(2,1)}) %all-gather.11.cloned.1.call-update) | async-done | bytes 3276816 | tf_op jit(solution)/shard_map/all_gather | solution.py:54
  522.1 39.6 %all-gather.13.cloned.1.call-done = bf16[640,2560]{1,0:T(8,128)(2,1)} async-done(((bf16[80,2560]{1,0:T(8,128)(2,1)}), bf16[640,2560]{1,0:T(8,128)(2,1)}) %all-gather.13.cloned.1.call-update) | async-done | bytes 3276816 | tf_op jit(solution)/shard_map/all_gather | solution.py:54
  561.7 6.3 pad_maximum_fusion.1
  568.0 33.4 %all-gather.7.cloned.1.call-done = bf16[640,2560]{1,0:T(8,128)(2,1)} async-done(((bf16[80,2560]{1,0:T(8,128)(2,1)}), bf16[640,2560]{1,0:T(8,128)(2,1)}) %all-gather.7.cloned.1.call-update) | async-done | bytes 3276816 | tf_op jit(solution)/shard_map/all_gather | solution.py:54
  601.4 39.6 %all-gather.9.cloned.1.call-done = bf16[640,2560]{1,0:T(8,128)(2,1)} async-done(((bf16[80,2560]{1,0:T(8,128)(2,1)}), bf16[640,2560]{1,0:T(8,128)(2,1)}) %all-gather.9.cloned.1.call-update) | async-done | bytes 3276816 | tf_op jit(solution)/shard_map/all_gather | solution.py:54
  641.0 6.3 pad_maximum_fusion
  (65 shorter events, 0.6 us)
Async XLA Ops:
  7.2 264.5 %reduce-scatter.17.cloned.1.call-start = ((), (), s32[]{:S(2)}) async-start(), calls=%async_computation.16 | async-start | bytes 3686400 | tf_op jit(solution)/shard_map/reduce_scatter | solution.py:49
  10.2 39.4 %copy-start = (bf16[1,2048,640]{1,2,0:T(8,128)(2,1)}, bf16[1,2048,640]{1,2,0:T(8,128)(2,1)S(1)}, u32[]{:S(2)}) copy-start(bf16[1,2048,640]{1,2,0:T(8,128)(2,1)S(1)} %copy.20) | copy-start | bytes 7864324
  10.8 15.3 %copy-start.17 = (f32[2048]{0:T(1024)}, f32[2048]{0:T(1024)S(1)}, u32[]{:S(2)}) copy-start(f32[2048]{0:T(1024)S(1)} %add_rsqrt_fusion) | copy-start | bytes 24580
  10.8 38.8 %slice-start = ((s8[6553600]{0:T(1024)(128)(4,1)}), s8[4194304]{0:T(1024)(128)(4,1)S(1)}, s32[]{:S(2)}) async-start(s8[6553600]{0:T(1024)(128)(4,1)} %bitcast.188), calls=%async_computation.18 | async-start | bytes 8388608
  26.1 23.5 %slice-start.1 = ((s8[6553600]{0:T(1024)(128)(4,1)}), s8[2359296]{0:T(1024)(128)(4,1)S(1)}, s32[]{:S(2)}) async-start(s8[6553600]{0:T(1024)(128)(4,1)} %bitcast.188), calls=%async_computation.19 | async-start | bytes 4718592
  49.6 10.4 %copy-start.13 = (bf16[1,2048,640]{2,1,0:T(8,128)(2,1)S(1)}, bf16[1,2048,640]{2,1,0:T(8,128)(2,1)}, u32[]{:S(2)}) copy-start(bf16[1,2048,640]{2,1,0:T(8,128)(2,1)} %param.12) | copy-start | bytes 7864324
  59.9 10.9 %copy-start.15 = (f32[2048]{0:T(1024)}, f32[2048]{0:T(1024)S(1)}, u32[]{:S(2)}) copy-start(f32[2048]{0:T(1024)S(1)} %get-tuple-element.35) | copy-start | bytes 24580
  59.9 10.9 %copy-start.10 = (bf16[2048,640]{0,1:T(8,128)(2,1)}, bf16[2048,640]{0,1:T(8,128)(2,1)S(1)}, u32[]{:S(2)}) copy-start(bf16[2048,640]{0,1:T(8,128)(2,1)S(1)} %get-tuple-element.36) | copy-start | bytes 7864324
  84.2 31.3 %copy-start.14 = (bf16[1,2048,640]{2,1,0:T(8,128)(2,1)S(1)}, bf16[1,2048,640]{2,1,0:T(8,128)(2,1)}, u32[]{:S(2)}) copy-start(bf16[1,2048,640]{2,1,0:T(8,128)(2,1)} %param.12) | copy-start | bytes 7864324
  135.0 136.7 %reduce-scatter.15.cloned.1.call-start = ((), (), s32[]{:S(2)}) async-start(), calls=%async_computation.14 | async-start | bytes 3686400 | tf_op jit(solution)/shard_map/reduce_scatter | solution.py:49
  150.8 19.1 %copy-start.16 = (f32[2048]{0:T(1024)S(1)}, f32[2048]{0:T(1024)}, u32[]{:S(2)}) copy-start(f32[2048]{0:T(1024)} %copy-done.15) | copy-start | bytes 24580
  174.2 1.5 copy-start.12
  175.7 12.7 %copy-start.11 = (bf16[2048,640]{0,1:T(8,128)(2,1)S(1)}, bf16[2048,640]{0,1:T(8,128)(2,1)}, u32[]{:S(2)}) copy-start(bf16[2048,640]{0,1:T(8,128)(2,1)} %copy-done.10) | copy-start | bytes 7864324
  188.4 93.9 %reduce-scatter.13.cloned.1.call-start = ((), (), s32[]{:S(2)}) async-start(), calls=%async_computation.12 | async-start | bytes 3686400 | tf_op jit(solution)/shard_map/reduce_scatter | solution.py:49
  203.7 13.7 %copy-start.1 = (bf16[1,2048,640]{1,2,0:T(8,128)(2,1)S(1)}, bf16[1,2048,640]{1,2,0:T(8,128)(2,1)}, u32[]{:S(2)}) copy-start(bf16[1,2048,640]{1,2,0:T(8,128)(2,1)} %copy-done) | copy-start | bytes 7864324
  203.7 13.7 %copy-start.18 = (f32[2048]{0:T(1024)S(1)}, f32[2048]{0:T(1024)}, u32[]{:S(2)}) copy-start(f32[2048]{0:T(1024)} %copy-done.17) | copy-start | bytes 24580
  203.7 114.1 %reduce-scatter.11.cloned.1.call-start = ((), (), s32[]{:S(2)}) async-start(), calls=%async_computation.10 | async-start | bytes 3686400 | tf_op jit(solution)/shard_map/reduce_scatter | solution.py:49
  232.7 127.8 %reduce-scatter.9.cloned.1.call-start = ((), (), s32[]{:S(2)}) async-start(), calls=%async_computation.8 | async-start | bytes 3686400 | tf_op jit(solution)/shard_map/reduce_scatter | solution.py:49
  244.4 158.7 %reduce-scatter.7.cloned.1.call-start = ((), (), s32[]{:S(2)}) async-start(), calls=%async_computation.6 | async-start | bytes 3686400 | tf_op jit(solution)/shard_map/reduce_scatter | solution.py:49
  266.4 176.1 %all-gather.15.cloned.1.call-start = ((), (), s32[]{:S(2)}) async-start(), calls=%async_computation.15 | async-start | bytes 3686400 | tf_op jit(solution)/shard_map/all_gather | solution.py:54
  276.4 205.9 %all-gather.17.cloned.1.call-start = ((), (), s32[]{:S(2)}) async-start(), calls=%async_computation.17 | async-start | bytes 3686400 | tf_op jit(solution)/shard_map/all_gather | solution.py:54
  277.1 244.9 %all-gather.11.cloned.1.call-start = ((), (), s32[]{:S(2)}) async-start(), calls=%async_computation.11 | async-start | bytes 3686400 | tf_op jit(solution)/shard_map/all_gather | solution.py:54
  322.5 239.2 %all-gather.13.cloned.1.call-start = ((), (), s32[]{:S(2)}) async-start(), calls=%async_computation.13 | async-start | bytes 3686400 | tf_op jit(solution)/shard_map/all_gather | solution.py:54
  323.1 278.3 %all-gather.7.cloned.1.call-start = ((), (), s32[]{:S(2)}) async-start(), calls=%async_computation.7 | async-start | bytes 3686400 | tf_op jit(solution)/shard_map/all_gather | solution.py:54
  407.8 4.8 copy-start.2
  407.8 4.8 copy-start.3
  407.8 4.8 copy-start.4
  407.8 4.8 copy-start.5
  407.8 233.2 %all-gather.9.cloned.1.call-start = ((), (), s32[]{:S(2)}) async-start(), calls=%async_computation.9 | async-start | bytes 3686400 | tf_op jit(solution)/shard_map/all_gather | solution.py:54
  408.4 6.2 copy-start.6
  408.4 6.2 copy-start.7
  408.4 6.2 copy-start.8
  408.5 6.2 copy-start.9
Sparse Core Ops, SparseCore 0:
  135.1 43.8 reduce-scatter.16
  188.5 43.8 reduce-scatter.14
  234.7 39.8 reduce-scatter.12
  277.3 40.4 reduce-scatter.10
  320.5 39.8 reduce-scatter.8
  363.2 39.8 reduce-scatter.6
  404.8 37.7 all-gather.14
  444.2 38.0 all-gather.16
  483.9 38.0 all-gather.10
  523.5 38.0 all-gather.12
  563.3 38.0 all-gather.6
  602.9 38.0 all-gather.8

commit v2 on v1

v2 whole, which is shorter than its diff:
```python
import functools

import jax
import jax.numpy as jnp
from jax import lax
from jax.experimental import pallas as pl
from jax.experimental.pallas import tpu as pltpu
from jax.sharding import PartitionSpec as P

MESH = pl.DeviceIdType.MESH
BF = jnp.bfloat16
F32 = jnp.float32
T, D, FF = 2048, 640, 2560
C = 256
S = 128
NL = 10
NG = 20
TILE = 512
EPS = 1e-6
OWN = 4
SCHEDULE = (
    ("partner", 1), ("sum", 0, 3, 1), ("sum", 0, 2, 1), ("sum", 0, 1, 1), ("sum", 1, 3, 4), ("sum", 1, 2, 4), ("sum", 2, 3, 7),
    ("final", 1, 7), ("final", 0, 10), ("sent", 10),
    ("gather", 2, 1, 10), ("gather", 1, 0, 14), ("gather", 3, 1, 13), ("gather", 2, 0, 17), ("gather", 3, 0, 20), ("gather", 3, 2, 12),
)
LAST = max((3 + one[-1]) // 4 for one in SCHEDULE)


def chunk_of(i):
    pair, t = i % 2, i // 2
    low = t <= 2
    z1, s1 = jnp.where(low, pair, 3 - pair), jnp.where(low, t, 4 - t)
    z2, s2 = jnp.where(low, 3 - pair, pair), jnp.where(low, 4 - t, t)
    return t, z1, s1, z2, s2


def strips_of(i):
    _, z1, s1, z2, s2 = chunk_of(i)
    return pl.multiple_of(640 * z1 + S * s1, S), pl.multiple_of(640 * z2 + S * s2, S)


def down_piece(i, c, k):
    t, z1, s1, z2, s2 = chunk_of(i)
    mid = t == 2
    dest = jnp.where(mid, z1 if k == 0 else z2, jnp.where(c == 0, z1, z2))
    s = jnp.where(c == 0, s1, s2)
    off = jnp.where(mid, jnp.where(c == 0, 256, 0), 64 * (2 * s + k - 5 * c))
    return dest, pl.multiple_of(off, 64)


def norm_of(h):
    wide = h.astype(F32)
    scale = lax.rsqrt(jnp.mean(wide * wide, -1, keepdims=True) + EPS)
    return wide, scale


def dot(a, b):
    return jnp.dot(a, b, preferred_element_type=F32)


def dot_t(a, b):
    return lax.dot_general(a, b, (((1,), (1,)), ((), ())), preferred_element_type=F32)


def adamw(w, m, v, g):
    m = 0.9 * m + 0.1 * g
    v = 0.95 * v + 0.05 * g * g
    step = m * lax.rsqrt(v + 1e-8) + 0.1 * w
    return (w - 0.02 * step).astype(BF), m, v


def kernel(
    x_h, dy_h, wg_h, wu_h, wd_h, mg_h, mu_h, md_h, vg_h, vu_h, vd_h,
    nwg, nwd, omg, omu, omd, ovg, ovu, ovd,
    H, A, AT, Y, YT, ACC, HID, DG, DU, WG, WU, WD, own_g, own_d, p_g, p_d, r_g, r_d,
    st_mg, st_vg, st_wg, st_md, st_vd, st_wd,
    sem_in, sem_w, sem_ld, sem_st, sem_send, sem_loc, sem_own, sem_pg, sem_pd, sem_rg, sem_rd, sem_ag, sem_ad, sem_pa,
):
    rep, dp = lax.axis_index("rep"), lax.axis_index("dp")
    z, c = dp // 2, dp % 2
    is_end = (z == 0) | (z == 3)
    is_mid = (z == 1) | (z == 2)

    def to(dz, flip=False):
        return (rep, (z + dz) * 2 + ((1 - c) if flip else c))

    barrier = pltpu.get_barrier_semaphore()
    pl.semaphore_signal(barrier, inc=1, device_id=to(0, True), device_id_type=MESH)

    @pl.when(z > 0)
    def _():
        pl.semaphore_signal(barrier, inc=1, device_id=to(-1), device_id_type=MESH)

    @pl.when(z < 3)
    def _():
        pl.semaphore_signal(barrier, inc=1, device_id=to(1), device_id_type=MESH)

    def w_copies(n):
        layer = jnp.where((n >= 10) & (n < 20), 1, 0)
        f1, f2 = strips_of(n % NL)
        slot = n % 2
        out = []
        for k, f in enumerate((f1, f2)):
            out.append(functools.partial(pltpu.make_async_copy, wg_h.at[layer, :, pl.ds(f, S)], WG.at[slot, :, pl.ds(S * k, S)], sem_w.at[slot, k]))
            out.append(functools.partial(pltpu.make_async_copy, wu_h.at[layer, :, pl.ds(f, S)], WU.at[slot, :, pl.ds(S * k, S)], sem_w.at[slot, 2 + k]))
            out.append(functools.partial(pltpu.make_async_copy, wd_h.at[layer, pl.ds(f, S), :], WD.at[slot, pl.ds(S * k, S), :], sem_w.at[slot, 4 + k]))
        return out

    def w_start(n):
        for one in w_copies(n):
            one().start()

    def w_wait(n):
        for one in w_copies(n):
            one().wait()

    def st_copies(g):
        slot = g % 2
        layer = 1 - g // NL
        i = g % NL
        f = strips_of(i)
        loads, stores = [], []
        for q, (m_h, v_h, w_h, om, ov) in enumerate(((mg_h, vg_h, wg_h, omg, ovg), (mu_h, vu_h, wu_h, omu, ovu))):
            for k in range(2):
                at = pl.ds(f[k], S)
                j = 2 * q + k
                loads.append(functools.partial(pltpu.make_async_copy, m_h.at[layer, :, at], st_mg.at[slot, j], sem_ld.at[slot, 0, j]))
                loads.append(functools.partial(pltpu.make_async_copy, v_h.at[layer, :, at], st_vg.at[slot, j], sem_ld.at[slot, 1, j]))
                rows = pl.ds(pl.multiple_of(80 * dp, 80), 80)
                loads.append(functools.partial(pltpu.make_async_copy, w_h.at[layer, rows, at], st_wg.at[slot, j], sem_ld.at[slot, 2, j]))
                stores.append(functools.partial(pltpu.make_async_copy, st_mg.at[slot, j], om.at[layer, :, at], sem_st.at[slot, 0, j]))
                stores.append(functools.partial(pltpu.make_async_copy, st_vg.at[slot, j], ov.at[layer, :, at], sem_st.at[slot, 1, j]))
        out = [(None, loads, stores)]
        for k in range(2):
            dest, off = down_piece(i, c, k)
            at = pl.ds(off, 64)
            rows = pl.ds(pl.multiple_of(320 * dp + off, 64), 64)
            loads = [
                functools.partial(pltpu.make_async_copy, md_h.at[layer, at], st_md.at[slot, k], sem_ld.at[slot, 0, 4 + k]),
                functools.partial(pltpu.make_async_copy, vd_h.at[layer, at], st_vd.at[slot, k], sem_ld.at[slot, 1, 4 + k]),
                functools.partial(pltpu.make_async_copy, wd_h.at[layer, rows], st_wd.at[slot, k], sem_ld.at[slot, 2, 4 + k]),
            ]
            stores = [
                functools.partial(pltpu.make_async_copy, st_md.at[slot, k], omd.at[layer, at], sem_st.at[slot, 0, 4 + k]),
                functools.partial(pltpu.make_async_copy, st_vd.at[slot, k], ovd.at[layer, at], sem_st.at[slot, 1, 4 + k]),
            ]
            out.append((dest == z, loads, stores))
        return out

    def st_do(g, which, act):
        for cond, *lists in st_copies(g):
            def go(copies=lists[which]):
                for one in copies:
                    getattr(one(), act)()
            if cond is None:
                go()
            else:
                pl.when(cond)(go)

    def rs_copy_g(g, j, dz):
        to_dest = (dz == -1) & (j == z - 1)
        slot = jnp.where(to_dest, 4, j)
        return pltpu.make_async_remote_copy(
            p_g.at[g, j], r_g.at[g, slot], sem_send.at[0], sem_rg.at[g, slot], device_id=to(dz), device_id_type=MESH)

    def rs_copy_d(g, k, dz):
        side = jnp.where(dz == 1, 0, 1)
        return pltpu.make_async_remote_copy(
            p_d.at[g, k], r_d.at[g, k, side], sem_send.at[1], sem_rd.at[g, k, side], device_id=to(dz), device_id_type=MESH)

    def wait_rg(g, slot):
        pltpu.make_async_remote_copy(
            p_g.at[g, 0], r_g.at[g, slot], sem_send.at[0], sem_rg.at[g, slot], device_id=to(0, True), device_id_type=MESH).wait_recv()

    def wait_rd(g, k, side):
        pltpu.make_async_remote_copy(
            p_d.at[g, k], r_d.at[g, k, side], sem_send.at[1], sem_rd.at[g, k, side], device_id=to(0, True), device_id_type=MESH).wait_recv()

    def ag_start_g(g, d, src, dz):
        pltpu.make_async_remote_copy(
            src, nwg.at[g, c, d], sem_send.at[2], sem_ag.at[g, d], device_id=to(dz), device_id_type=MESH).start()

    def ag_start_d(g, k, src, dz):
        pltpu.make_async_remote_copy(
            src, nwd.at[g, c, k], sem_send.at[3], sem_ad.at[g, k], device_id=to(dz), device_id_type=MESH).start()

    def partner_start_g(g, d, src):
        pltpu.make_async_remote_copy(
            src, nwg.at[g, c, d], sem_send.at[4], sem_pa.at[0], device_id=to(0, True), device_id_type=MESH).start()

    def partner_start_d(g, k, src):
        pltpu.make_async_remote_copy(
            src, nwd.at[g, c, k], sem_send.at[5], sem_pa.at[1], device_id=to(0, True), device_id_type=MESH).start()

    def wait_ag(g, d):
        pltpu.make_async_remote_copy(
            nwg.at[g, c, d], nwg.at[g, c, d], sem_send.at[2], sem_ag.at[g, d], device_id=to(0, True), device_id_type=MESH).wait_recv()

    def wait_ad(g, k):
        pltpu.make_async_remote_copy(
            nwd.at[g, c, k], nwd.at[g, c, k], sem_send.at[3], sem_ad.at[g, k], device_id=to(0, True), device_id_type=MESH).wait_recv()

    def own_copies(g):
        slot = g % OWN
        return (
            functools.partial(pltpu.make_async_remote_copy,
                own_g.at[slot, 1 - c], p_g.at[g], sem_own.at[slot, 0], sem_pg.at[g], device_id=to(0, True), device_id_type=MESH),
            functools.partial(pltpu.make_async_remote_copy,
                own_d.at[slot, 1 - c], p_d.at[g], sem_own.at[slot, 1], sem_pd.at[g], device_id=to(0, True), device_id_type=MESH),
        )

    def sum_g(g, j, *slots):
        out = own_g[g % OWN, c, j].astype(F32) + p_g[g, j].astype(F32)
        for slot in slots:
            out = out + r_g[g, slot].astype(F32)
        return out.astype(BF)

    def sum_d(g, k, *sides):
        out = own_d[g % OWN, c, k].astype(F32) + p_d[g, k].astype(F32)
        for side in sides:
            out = out + r_d[g, k, side].astype(F32)
        return out.astype(BF)

    def dest_of(g, k):
        return down_piece(g % NL, c, k)[0]

    def final(g, both):
        slot = g % 2
        st_do(g, 0, "wait")
        if both:
            wait_rg(g, z)
            wait_rg(g, 4)
            total = sum_g(g, z, z, 4)
        else:
            r = jnp.where(z == 0, 4, z)
            wait_rg(g, r)
            total = sum_g(g, z, r)
        for j in range(4):
            rows, cols = slice(80 * (j // 2), 80 * (j // 2) + 80), slice(S * (j % 2), S * (j % 2) + S)
            new, m, v = adamw(st_wg[slot, j].astype(F32), st_mg[slot, j], st_vg[slot, j], total[rows, cols].astype(F32))
            p_g[g, z, rows, cols] = new
            st_mg[slot, j] = m
            st_vg[slot, j] = v
        here = p_g.at[g, z]
        if both:
            ag_start_g(g, z, here, 1)
            ag_start_g(g, z, here, -1)
        else:
            ag_start_g(g, z, here, jnp.where(z == 0, 1, -1))
        partner_start_g(g, z, here)
        pltpu.make_async_copy(here, nwg.at[g, c, z], sem_loc).start()
        for k in range(2):
            d = dest_of(g, k)

            @pl.when(d == z)
            def _():
                if both:
                    wait_rd(g, k, 0)
                    wait_rd(g, k, 1)
                    total = sum_d(g, k, 0, 1)
                else:
                    side = jnp.where(z == 0, 1, 0)
                    wait_rd(g, k, side)
                    total = sum_d(g, k, side)
                new, m, v = adamw(st_wd[slot, k].astype(F32), st_md[slot, k], st_vd[slot, k], total.astype(F32))
                p_d[g, k] = new
                st_md[slot, k] = m
                st_vd[slot, k] = v
                here = p_d.at[g, k]
                if both:
                    ag_start_d(g, k, here, 1)
                    ag_start_d(g, k, here, -1)
                else:
                    ag_start_d(g, k, here, jnp.where(z == 0, 1, -1))
                partner_start_d(g, k, here)
                pltpu.make_async_copy(here, nwd.at[g, c, k], sem_loc).start()

        st_do(g, 1, "start")

        @pl.when(g + 1 < NG)
        def _():
            @pl.when(g >= 1)
            def _():
                st_do(g - 1, 1, "wait")
            st_do(g + 1, 0, "start")

    def mirrored(rz, rd):
        plain = z == rz
        return plain | (z == 3 - rz), jnp.where(plain, rd, 3 - rd), jnp.where(plain, 1, -1), jnp.where(plain, 0, 1)

    def reduce_step(g, rz, rd):
        active, d, dz, side = mirrored(rz, rd)

        @pl.when(active)
        def _():
            if rz == 0:
                p_g[g, d] = sum_g(g, d)
            else:
                wait_rg(g, d)
                p_g[g, d] = sum_g(g, d, d)
            rs_copy_g(g, d, dz).start()
            for k in range(2):
                @pl.when(dest_of(g, k) == d)
                def _():
                    if rz == 0:
                        p_d[g, k] = sum_d(g, k)
                    else:
                        wait_rd(g, k, side)
                        p_d[g, k] = sum_d(g, k, side)
                    rs_copy_d(g, k, dz).start()

    def final_step(g, rz):
        pl.when((z == rz) | (z == 3 - rz))(lambda: final(g, rz == 1))

    def gather_step(g, rz, rd):
        active, d, dz, _ = mirrored(rz, rd)

        @pl.when(active)
        def _():
            wait_ag(g, d)
            here = nwg.at[g, c, d]
            if rz < 3:
                ag_start_g(g, d, here, dz)
            partner_start_g(g, d, here)
            for k in range(2):
                @pl.when(dest_of(g, k) == d)
                def _():
                    wait_ad(g, k)
                    here = nwd.at[g, c, k]
                    if rz < 3:
                        ag_start_d(g, k, here, dz)
                    partner_start_d(g, k, here)

    def partner_step(g):
        for one in own_copies(g):
            one().wait_recv()

    def own_sent(g):
        for one in own_copies(g):
            one().wait_send()

    steps = {"partner": partner_step, "sum": reduce_step, "final": final_step, "gather": gather_step, "sent": own_sent}

    def tick(it, s):
        todo = [((3 + o) // 4, n, step) for n, (*step, o) in enumerate(SCHEDULE) if (3 + o) % 4 == s]
        for lag, _, (name, *rest) in sorted(todo, key=lambda one: (-one[0], one[1])):
            when_chunk(it - lag, functools.partial(lambda g, name, rest: steps[name](g, *rest), name=name, rest=rest))

    def when_chunk(g, fn):
        pl.when((g >= 0) & (g < NG))(lambda: fn(g))

    x_in = pltpu.make_async_copy(x_h, H, sem_in.at[0])
    y_in = pltpu.make_async_copy(dy_h, Y, sem_in.at[1])
    x_in.start()
    y_in.start()
    w_start(0)
    st_do(0, 0, "start")
    ROWS = 256

    def norm_rows(i):
        rows = pl.ds(pl.multiple_of(i * ROWS, ROWS), ROWS)
        wide, scale = norm_of(H[rows, :])
        a = (wide * scale).astype(BF)
        A[rows, :] = a
        return rows, a

    x_in.wait()

    @pl.loop(0, T // ROWS)
    def _(i):
        rows, _ = norm_rows(i)
        ACC[rows, :] = jnp.zeros((ROWS, D), F32)

    @pl.loop(0, NL)
    def _(n):
        slot = n % 2
        w_wait(n)
        w_start(n + 1)

        @pl.loop(0, T // TILE)
        def _(i):
            rows = pl.ds(pl.multiple_of(i * TILE, TILE), TILE)
            a = A[rows, :]
            gate = dot(a, WG[slot])
            up = dot(a, WU[slot])
            hid = (gate * jax.nn.sigmoid(gate) * up).astype(BF)
            ACC[rows, :] += dot(hid, WD[slot])

    y_in.wait()

    @pl.loop(0, T // ROWS)
    def _(i):
        rows = pl.ds(pl.multiple_of(i * ROWS, ROWS), ROWS)
        H[rows, :] = (H[rows, :].astype(F32) + ACC[rows, :].astype(BF).astype(F32)).astype(BF)
        rows, a = norm_rows(i)
        AT[:, rows] = a.T
        YT[:, rows] = Y[rows, :].T
        ACC[rows, :] = jnp.zeros((ROWS, D), F32)

    pl.semaphore_wait(barrier, 1 + jnp.where(z > 0, 1, 0) + jnp.where(z < 3, 1, 0))

    def between_layers():
        @pl.loop(0, T // ROWS)
        def _(i):
            rows = pl.ds(pl.multiple_of(i * ROWS, ROWS), ROWS)
            wide, scale = norm_of(H[rows, :])
            ct = ACC[rows, :].astype(BF).astype(F32)
            by_scale = jnp.sum(ct * wide, -1, keepdims=True)
            by_h = ct * scale - wide * (by_scale * scale * scale * scale * (1.0 / D))
            y = (Y[rows, :].astype(F32) + by_h.astype(BF).astype(F32)).astype(BF)
            Y[rows, :] = y
            YT[:, rows] = y.T

        x_again = pltpu.make_async_copy(x_h, H, sem_in.at[0])
        x_again.start()
        x_again.wait()

        @pl.loop(0, T // ROWS)
        def _(i):
            rows, a = norm_rows(i)
            AT[:, rows] = a.T

    def tiles(g, first, last):
        slot = g % 2

        @pl.loop(first, last)
        def _(i):
            rows = pl.ds(pl.multiple_of(i * TILE, TILE), TILE)
            a = A[rows, :]
            gate = dot(a, WG[slot])
            up = dot(a, WU[slot])
            by_hid = dot_t(Y[rows, :], WD[slot]).astype(BF).astype(F32)
            sig = jax.nn.sigmoid(gate)
            silu = gate * sig
            HID[rows, :] = (silu * up).astype(BF)
            DU[rows, :] = (by_hid * silu).astype(BF)
            DG[rows, :] = (by_hid * up * (sig + silu * (1.0 - sig))).astype(BF)

            @pl.when(g < NL)
            def _():
                ACC[rows, :] += dot_t(DG[rows, :], WG[slot]) + dot_t(DU[rows, :], WU[slot])

    def weight_grad(g, src, q):
        slot = g % OWN
        out = dot(AT[...], src[...]).astype(BF)
        for b in range(8):
            own_g[slot, b % 2, b // 2, 80 * q : 80 * q + 80, :] = out[80 * b : 80 * b + 80, :]

    def down_grad(g):
        slot = g % OWN
        out = dot(YT[...], HID[...]).T.astype(BF)
        mid = (g % NL) // 2 == 2
        for strip in range(2):
            for half in range(2):
                core = jnp.where(mid, half, strip)
                k = jnp.where(mid, strip, half)
                row = S * strip + 64 * half
                own_d[slot, core, k] = out[row : row + 64, :]

    @pl.loop(0, NG + LAST)
    def _(g):
        here = g < NG

        @pl.when(here)
        def _():
            w_wait(g + 10)
            pl.when(g + 1 < NG)(lambda: w_start(g + 11))
            pl.when(g == NL)(between_layers)
            tiles(g, 0, 2)

        tick(g, 0)
        pl.when(here)(lambda: tiles(g, 2, 4))
        tick(g, 1)

        @pl.when(here)
        def _():
            weight_grad(g, DG, 0)
            weight_grad(g, DU, 1)
            own_copies(g)[0]().start()

        tick(g, 2)

        @pl.when(here)
        def _():
            down_grad(g)
            own_copies(g)[1]().start()

        tick(g, 3)

    st_do(NG - 2, 1, "wait")
    st_do(NG - 1, 1, "wait")

    pltpu.make_async_copy(p_d.at[pl.ds(0, 15)], nwd.at[pl.ds(0, 15), c], sem_loc).wait()

    def all_of(ref, send, recv):
        return pltpu.make_async_remote_copy(ref, ref, send, recv, device_id=to(0, True), device_id_type=MESH)

    all_of(nwg.at[:, 1 - c], sem_send.at[4], sem_pa.at[0]).wait_recv()
    all_of(nwd.at[:, 1 - c], sem_send.at[5], sem_pa.at[1]).wait_recv()

    def sent(which, ref):
        all_of(ref, sem_send.at[which], sem_pa.at[0]).wait_send()

    sent(0, r_g.at[:, pl.ds(0, 3)])
    sent(1, p_d.at[pl.ds(0, 15)])
    sent(4, nwg.at[:, c])
    sent(5, nwd.at[:, c])

    @pl.when(is_end)
    def _():
        sent(2, r_g.at[:, 0])
        sent(3, p_d.at[pl.ds(0, 5)])

    @pl.when(is_mid)
    def _():
        sent(2, r_g)
        sent(3, r_g.at[pl.ds(0, 10)])


def train(x, dy, *arrays):
    anyspace = pl.BlockSpec(memory_space=pl.ANY)
    sds = jax.ShapeDtypeStruct
    dma = pltpu.SemaphoreType.DMA
    vm = pltpu.VMEM
    outs = (
        sds((NG, 2, 4, 160, C), BF), sds((NG, 2, 2, 64, D), BF),
        sds((2, 80, FF), F32), sds((2, 80, FF), F32), sds((2, 320, D), F32),
        sds((2, 80, FF), F32), sds((2, 80, FF), F32), sds((2, 320, D), F32),
    )
    return pl.pallas_call(
        kernel,
        out_shape=outs,
        in_specs=[anyspace] * 11,
        out_specs=(anyspace,) * 8,
        scratch_shapes=[
            vm((T, D), BF), vm((T, D), BF), vm((D, T), BF), vm((T, D), BF), vm((D, T), BF), vm((T, D), F32),
            vm((T, C), BF), vm((T, C), BF), vm((T, C), BF),
            vm((2, D, C), BF), vm((2, D, C), BF), vm((2, C, D), BF),
            vm((OWN, 2, 4, 160, C), BF), vm((OWN, 2, 2, 64, D), BF),
            vm((NG, 4, 160, C), BF), vm((NG, 2, 64, D), BF), vm((NG, 5, 160, C), BF), vm((NG, 2, 2, 64, D), BF),
            vm((2, 4, 80, S), F32), vm((2, 4, 80, S), F32), vm((2, 4, 80, S), BF),
            vm((2, 2, 64, D), F32), vm((2, 2, 64, D), F32), vm((2, 2, 64, D), BF),
            dma((2,)), dma((2, 6)), dma((2, 3, 6)), dma((2, 2, 6)), dma((6,)), dma, dma((OWN, 2)), dma((NG,)), dma((NG,)),
            dma((NG, 5)), dma((NG, 2, 2)), dma((NG, 4)), dma((NG, 2)), dma((2,)),
        ],
        compiler_params=pltpu.CompilerParams(
            collective_id=0, has_side_effects=True, vmem_limit_bytes=67000000),
        name="train",
    )(x, dy, *arrays)


def place(nwg, nwd, wg, wu, wd, buf_g, buf_d, sem_g, sem_d, sem_out):
    def load(g):
        return (
            functools.partial(pltpu.make_async_copy, nwg.at[g], buf_g.at[g], sem_g.at[g]),
            functools.partial(pltpu.make_async_copy, nwd.at[g], buf_d.at[g], sem_d.at[g]),
        )

    def store(g, act):
        layer, i = 1 - g // NL, g % NL
        f = strips_of(i)

        @pl.loop(0, 8)
        def _(b):
            rows = pl.ds(pl.multiple_of(80 * b, 80), 80)
            for q, out in enumerate((wg, wu)):
                for k in range(2):
                    src = buf_g.at[g, b % 2, b // 2, pl.ds(80 * q, 80), pl.ds(S * k, S)]
                    getattr(pltpu.make_async_copy(src, out.at[layer, rows, pl.ds(f[k], S)], sem_out.at[0]), act)()

        for core in range(2):
            for k in range(2):
                dest, off = down_piece(i, core, k)
                rows = pl.ds(pl.multiple_of(640 * dest + 320 * core + off, 64), 64)
                getattr(pltpu.make_async_copy(buf_d.at[g, core, k], wd.at[layer, rows], sem_out.at[1]), act)()

    @pl.loop(0, NG)
    def _(g):
        for one in load(g):
            one().start()

    @pl.loop(0, NG)
    def _(g):
        for one in load(g):
            one().wait()
        store(g, "start")

    @pl.loop(0, NG)
    def _(g):
        store(g, "wait")


def relayout(nwg, nwd):
    anyspace = pl.BlockSpec(memory_space=pl.ANY)
    sds = jax.ShapeDtypeStruct
    dma = pltpu.SemaphoreType.DMA
    return pl.pallas_call(
        place,
        out_shape=(sds((2, D, FF), BF), sds((2, D, FF), BF), sds((2, FF, D), BF)),
        in_specs=[anyspace] * 2,
        out_specs=(anyspace,) * 3,
        scratch_shapes=[
            pltpu.VMEM((NG, 2, 4, 160, C), BF), pltpu.VMEM((NG, 2, 2, 64, D), BF), dma((NG,)), dma((NG,)), dma((2,)),
        ],
        compiler_params=pltpu.CompilerParams(vmem_limit_bytes=50000000),
        name="place",
    )(nwg, nwd)


def solution(mesh):
    def step(x, dy, *arrays):
        nwg, nwd, *moments = train(x[0], dy[0], *arrays)
        return (*relayout(nwg, nwd), *moments)

    whole = P(None, None, None)
    rows = P(None, "dp", None)
    seq = P(("rep", "dp"), None, None)
    return jax.shard_map(
        step,
        mesh=mesh,
        in_specs=(seq, seq) + (whole,) * 3 + (rows,) * 6,
        out_specs=(P("rep", None, None),) * 3 + (P("rep", "dp", None),) * 6,
        check_vma=False,
    )
```

time: 663 us -> 326 us (0.49); the launches traced: 655 us -> 325 us
  waiting for transfers between devices: 324 us -> 0 us
  Pallas kernels: 0 us -> 310 us
  matrix products: 246 us -> 0 us
  other arithmetic: 45.9 us -> 0 us
  between operations: 14.9 us -> 0.69 us
  local copies, waits for them, and re-layouts: 23 us -> 14.1 us
    pallas_call x0 -> x2, Pallas kernels: none -> 310 us  [the longest x1 299 us: train(): pl.pallas_call(kernel, out_shape=outs, in_specs=[anyspace] * 11, out_spec...]
    dot_general x15 -> x0, matrix products: 246 us -> none  [the longest x5 92.9 us: layer(): gate = jnp.dot(a, w['w_gate'], preferred_element_type=jnp.float32)]
    all_gather x6 -> x0, waiting for transfers between devices: 212 us -> none  [step(): new[k, number] = (lax.all_gather(one, 'dp', axis=0, tiled=True), m1, v1)]
    reduce_scatter x6 -> x0, waiting for transfers between devices: 110 us -> none  [step(): g = lax.psum_scatter(by_w[NAMES[k]], 'dp', scatter_dimension=0, tiled=True)]
    another operation x6 -> x0, other arithmetic: 27.1 us -> none  [step(): jnp.stack([new[k, number][which] for number in range(layers)])]
    slice x3 -> x0, local copies, waits for them, and re-layouts: 15.4 us -> none  [the longest x2 10.3 us: step(): w[number]]
    convert_element_type x3 -> x0, other arithmetic: 14 us -> none  [adamw(): return ((w - 0.02 * step).astype(jnp.bfloat16), m, v)]
    unnamed x44 -> x20, local copies, waits for them, and re-layouts: 7.58 us -> 14.1 us
  transfers between devices with their start and end apart: 12 -> 0, of which waited for: 9 -> 0; matrix products, arithmetic and copies ran while one was open for 27% -> 0% of each run, Pallas kernels for 0% -> 0%
where the time goes in v2:
time: 326 us; the launch traced here: 325 us
  Pallas kernels  310 us (95%)
  local copies, waits for them, and re-layouts  14.1 us (4%)
    pallas_call x1, Pallas kernels, train(): pl.pallas_call(kernel, out_shape=outs, in_specs=[anyspace] * 11, out_spec...  299 us
    unnamed x20, local copies, waits for them, and re-layouts  14.1 us
    pallas_call x1, Pallas kernels, relayout(): pl.pallas_call(place, out_shape=(sds((2, D, FF), BF), sds((2, D, FF), BF)...  10.9 us

profile of v2, /device:TPU:0, one launch (start us, length us, event | category | flops | bytes accessed | tf_op | source)
XLA Modules:
  0.0 325.2 jit_solution(1727098566484351899)
XLA Ops:
  0.6 299.4 %train.1 = (bf16[20,2,4,160,256]{4,3,2,1,0:T(8,128)(2,1)}, bf16[20,2,2,64,640]{4,3,2,1,0:T(8,128)(2,1)}, f32[2,80,2560]{2,1,0:T(8,128)}, f32[2,80,2560]{2,1,0:T(...) custom-call(bf16[2048,640]{1,0:T(8,128)(2,1)} %bitcast.2, ...), custom_call_target="tpu_custom_call" | custom-call | tf_op jit(solution)/shard_map/train/pallas_call | solution.py:530
  300.1 0.0 copy-start
  300.1 2.9 copy-done
  303.0 0.0 copy-start.6
  303.0 10.9 %place.1 = (bf16[2,640,2560]{2,1,0:T(8,128)(2,1)}, bf16[2,640,2560]{2,1,0:T(8,128)(2,1)}, bf16[2,2560,640]{2,1,0:T(8,128)(2,1)}) custom-call(bf16[20,2,4,160,256]{4,3,2,1,0:T(8,128)(2,1)} %get-tuple-element.20.nwg, bf16[20,2,2,64,640]{4,3,2,1,0:T(8,128)(2,1)S(1)} %copy-done), custom_call_target="tpu_custom_call" | custom-call | tf_op jit(solution)/shard_map/place/pallas_call | solution.py:597
  313.9 0.0 copy-done.6
  313.9 0.0 copy-start.5
  313.9 1.2 copy.26
  315.1 0.8 copy-done.5
  315.9 0.0 copy-start.4
  315.9 1.2 copy.27
  317.1 0.9 copy-done.4
  317.9 0.0 copy-start.3
  317.9 1.2 copy.28
  319.1 0.9 copy-done.3
  319.9 0.0 copy-start.2
  319.9 1.2 copy.29
  321.1 0.9 copy-done.2
  322.0 0.0 copy-start.1
  322.0 1.2 copy.30
  323.1 0.9 copy-done.1
  324.0 1.2 copy.31
Async XLA Ops:
  300.1 2.9 copy-start
  303.0 10.9 %copy-start.6 = (f32[2,80,2560]{2,1,0:T(8,128)S(1)}, f32[2,80,2560]{2,1,0:T(8,128)}, u32[]{:S(2)}) copy-start(f32[2,80,2560]{2,1,0:T(8,128)} %get-tuple-element.43) | copy-start | bytes 4915204
  313.9 2.0 copy-start.5
  315.9 2.0 copy-start.4
  317.9 2.0 copy-start.3
  319.9 2.0 copy-start.2
  322.0 2.0 copy-start.1

commit v3 on v1

v3 whole, which is shorter than its diff:
```python
import functools

import jax
import jax.numpy as jnp
from jax import lax
from jax.experimental import pallas as pl
from jax.experimental.pallas import tpu as pltpu
from jax.sharding import PartitionSpec as P

MESH = pl.DeviceIdType.MESH
BF = jnp.bfloat16
F32 = jnp.float32
T, D, FF = 2048, 640, 2560
C = 256
S = 128
NL = 10
NG = 20
TILE = 512
EPS = 1e-6
WS = 4
OWN = 4
PARTS = 5
FIRST = 2
SCHEDULE = (
    ("partner", "g", 0, 2), ("partner", "d", 0, 1), ("partner", "g", 1, 5), ("partner", "d", 1, 7),
    ("sum", "g", 0, 3, 2), ("sum", "d", 0, 3, 3), ("sum", "g", 0, 2, 2), ("sum", "d", 0, 2, 1), ("sum", "g", 0, 1, 6), ("sum", "d", 0, 1, 3),
    ("sum", "g", 1, 3, 5), ("sum", "d", 1, 3, 9), ("sum", "g", 1, 2, 6), ("sum", "d", 1, 2, 7), ("sum", "g", 2, 3, 9), ("sum", "d", 2, 3, 11),
    ("final", "g", 1, 9), ("final", "d", 1, 11), ("final", "g", 0, 14), ("final", "d", 0, 15), ("sent", 15),
    ("gather", "g", 2, 1, 12), ("gather", "d", 2, 1, 13), ("gather", "g", 1, 0, 17), ("gather", "d", 1, 0, 17),
    ("gather", "g", 3, 1, 19), ("gather", "d", 3, 1, 23), ("gather", "g", 2, 0, 20), ("gather", "d", 2, 0, 21),
    ("gather", "g", 3, 0, 26), ("gather", "d", 3, 0, 25), ("gather", "g", 3, 2, 21), ("gather", "d", 3, 2, 17),
)
LAST = max((FIRST + one[-1]) // PARTS for one in SCHEDULE)


def chunk_of(i):
    pair, t = i % 2, i // 2
    low = t <= 2
    z1, s1 = jnp.where(low, pair, 3 - pair), jnp.where(low, t, 4 - t)
    z2, s2 = jnp.where(low, 3 - pair, pair), jnp.where(low, 4 - t, t)
    return t, z1, s1, z2, s2


def strips_of(i):
    _, z1, s1, z2, s2 = chunk_of(i)
    return pl.multiple_of(640 * z1 + S * s1, S), pl.multiple_of(640 * z2 + S * s2, S)


def down_piece(i, c, k):
    t, z1, s1, z2, s2 = chunk_of(i)
    mid = t == 2
    dest = jnp.where(mid, z1 if k == 0 else z2, jnp.where(c == 0, z1, z2))
    s = jnp.where(c == 0, s1, s2)
    off = jnp.where(mid, jnp.where(c == 0, 256, 0), 64 * (2 * s + k - 5 * c))
    return dest, pl.multiple_of(off, 64)


def norm_of(h):
    wide = h.astype(F32)
    scale = lax.rsqrt(jnp.mean(wide * wide, -1, keepdims=True) + EPS)
    return wide, scale


def dot(a, b):
    return jnp.dot(a, b, preferred_element_type=F32)


def dot_t(a, b):
    return lax.dot_general(a, b, (((1,), (1,)), ((), ())), preferred_element_type=F32)


def adamw(w, m, v, g):
    m = 0.9 * m + 0.1 * g
    v = 0.95 * v + 0.05 * g * g
    step = m * lax.rsqrt(v + 1e-8) + 0.1 * w
    return (w - 0.02 * step).astype(BF), m, v


def kernel(
    x_h, dy_h, wg_h, wu_h, wd_h, mg_h, mu_h, md_h, vg_h, vu_h, vd_h,
    nwg, nwd, omg, omu, omd, ovg, ovu, ovd, a0_h, a0t_h, h1_h,
    HS, A, AT, Y, YT, ACC, HID, DGU, WGU, WD, own_g, own_d, p_g, p_d, x_g, x_d,
    st_mg, st_vg, st_wg, st_md, st_vd, st_wd,
    sem_in, sem_w, sem_ld, sem_st, sem_send, sem_hs, sem_own, sem_pg, sem_pd, sem_rg, sem_rd, sem_ag, sem_ad, sem_pa,
):
    rep, dp = lax.axis_index("rep"), lax.axis_index("dp")
    z, c = dp // 2, dp % 2
    is_end = (z == 0) | (z == 3)
    is_mid = (z == 1) | (z == 2)

    def to(dz, flip=False):
        return (rep, (z + dz) * 2 + ((1 - c) if flip else c))

    barrier = pltpu.get_barrier_semaphore()
    pl.semaphore_signal(barrier, inc=1, device_id=to(0, True), device_id_type=MESH)

    @pl.when(z > 0)
    def _():
        pl.semaphore_signal(barrier, inc=1, device_id=to(-1), device_id_type=MESH)

    @pl.when(z < 3)
    def _():
        pl.semaphore_signal(barrier, inc=1, device_id=to(1), device_id_type=MESH)

    def w_copies(n):
        layer = jnp.where((n >= 10) & (n < 20), 1, 0)
        slot = n % WS
        out = []
        for k, f in enumerate(strips_of(n % NL)):
            out.append(functools.partial(pltpu.make_async_copy, wg_h.at[layer, :, pl.ds(f, S)], WGU.at[slot, :, pl.ds(S * k, S)], sem_w.at[slot, k]))
            out.append(functools.partial(pltpu.make_async_copy, wu_h.at[layer, :, pl.ds(f, S)], WGU.at[slot, :, pl.ds(C + S * k, S)], sem_w.at[slot, 2 + k]))
            out.append(functools.partial(pltpu.make_async_copy, wd_h.at[layer, pl.ds(f, S), :], WD.at[slot, pl.ds(S * k, S), :], sem_w.at[slot, 4 + k]))
        return out

    def w_start(n):
        for one in w_copies(n):
            one().start()

    def w_wait(n):
        for one in w_copies(n):
            one().wait()

    def st_copies(g):
        slot = g % 2
        layer = 1 - g // NL
        i = g % NL
        f = strips_of(i)
        loads, stores = [], []
        for q, (m_h, v_h, w_h, om, ov) in enumerate(((mg_h, vg_h, wg_h, omg, ovg), (mu_h, vu_h, wu_h, omu, ovu))):
            for k in range(2):
                at = pl.ds(f[k], S)
                j = 2 * q + k
                loads.append(functools.partial(pltpu.make_async_copy, m_h.at[layer, :, at], st_mg.at[slot, j], sem_ld.at[slot, 0, j]))
                loads.append(functools.partial(pltpu.make_async_copy, v_h.at[layer, :, at], st_vg.at[slot, j], sem_ld.at[slot, 1, j]))
                rows = pl.ds(pl.multiple_of(80 * dp, 80), 80)
                loads.append(functools.partial(pltpu.make_async_copy, w_h.at[layer, rows, at], st_wg.at[slot, j], sem_ld.at[slot, 2, j]))
                stores.append(functools.partial(pltpu.make_async_copy, st_mg.at[slot, j], om.at[layer, :, at], sem_st.at[slot, 0, j]))
                stores.append(functools.partial(pltpu.make_async_copy, st_vg.at[slot, j], ov.at[layer, :, at], sem_st.at[slot, 1, j]))
        out = [(None, loads, stores)]
        for k in range(2):
            dest, off = down_piece(i, c, k)
            at = pl.ds(off, 64)
            rows = pl.ds(pl.multiple_of(320 * dp + off, 64), 64)
            loads = [
                functools.partial(pltpu.make_async_copy, md_h.at[layer, at], st_md.at[slot, k], sem_ld.at[slot, 0, 4 + k]),
                functools.partial(pltpu.make_async_copy, vd_h.at[layer, at], st_vd.at[slot, k], sem_ld.at[slot, 1, 4 + k]),
                functools.partial(pltpu.make_async_copy, wd_h.at[layer, rows], st_wd.at[slot, k], sem_ld.at[slot, 2, 4 + k]),
            ]
            stores = [
                functools.partial(pltpu.make_async_copy, st_md.at[slot, k], omd.at[layer, at], sem_st.at[slot, 0, 4 + k]),
                functools.partial(pltpu.make_async_copy, st_vd.at[slot, k], ovd.at[layer, at], sem_st.at[slot, 1, 4 + k]),
            ]
            out.append((dest == z, loads, stores))
        return out

    def st_do(g, kind, which, act):
        for cond, *lists in st_copies(g):
            if (cond is None) != (kind == "g"):
                continue
            def go(copies=lists[which]):
                for one in copies:
                    getattr(one(), act)()
            if cond is None:
                go()
            else:
                pl.when(cond)(go)

    def remote(src, dst, send, recv, where):
        return pltpu.make_async_remote_copy(src, dst, send, recv, device_id=where, device_id_type=MESH)

    def rs_start_g(g, j, dz):
        to_end = (dz == -1) & (j == z - 1)

        @pl.when(to_end)
        def _():
            remote(p_g.at[g, j], x_g.at[g], sem_send.at[0], sem_rg.at[g, 4], to(-1)).start()

        @pl.when(jnp.logical_not(to_end))
        def _():
            remote(p_g.at[g, j], nwg.at[g, c, j], sem_send.at[0], sem_rg.at[g, j], to(dz)).start()

    def rs_start_d(g, k, d, dz):
        to_end = (dz == -1) & (d == z - 1)

        @pl.when(to_end)
        def _():
            remote(p_d.at[g, k], x_d.at[g // 2, k], sem_send.at[1], sem_rd.at[g, k, 1], to(-1)).start()

        @pl.when(jnp.logical_not(to_end))
        def _():
            side = jnp.where(dz == 1, 0, 1)
            remote(p_d.at[g, k], nwd.at[g, c, k], sem_send.at[1], sem_rd.at[g, k, side], to(dz)).start()

    def wait_rg(g, slot):
        remote(p_g.at[g, 0], x_g.at[g], sem_send.at[0], sem_rg.at[g, slot], to(0, True)).wait_recv()

    def wait_rd(g, k, side):
        remote(p_d.at[g, k], x_d.at[g // 2, k], sem_send.at[1], sem_rd.at[g, k, side], to(0, True)).wait_recv()

    def ag_start_g(g, d, dz):
        here = nwg.at[g, c, d]
        remote(here, here, sem_send.at[jnp.where(dz == 1, 2, 3)], sem_ag.at[g, d], to(dz)).start()

    def ag_start_d(g, k, dz):
        here = nwd.at[g, c, k]
        remote(here, here, sem_send.at[jnp.where(dz == 1, 4, 5)], sem_ad.at[g, k], to(dz)).start()

    def partner_start_g(g, d):
        here = nwg.at[g, c, d]
        remote(here, here, sem_send.at[6], sem_pa.at[0], to(0, True)).start()

    def partner_start_d(g, k):
        here = nwd.at[g, c, k]
        remote(here, here, sem_send.at[7], sem_pa.at[1], to(0, True)).start()

    def wait_ag(g, d):
        here = nwg.at[g, c, d]
        remote(here, here, sem_send.at[2], sem_ag.at[g, d], to(0, True)).wait_recv()

    def wait_ad(g, k):
        here = nwd.at[g, c, k]
        remote(here, here, sem_send.at[4], sem_ad.at[g, k], to(0, True)).wait_recv()

    def own_copies(g):
        slot = g % OWN
        return (
            functools.partial(pltpu.make_async_remote_copy,
                own_g.at[slot, 1 - c], p_g.at[g], sem_own.at[slot, 0], sem_pg.at[g], device_id=to(0, True), device_id_type=MESH),
            functools.partial(pltpu.make_async_remote_copy,
                own_d.at[slot, 1 - c], p_d.at[g], sem_own.at[slot, 1], sem_pd.at[g], device_id=to(0, True), device_id_type=MESH),
        )

    def sum_of(*terms):
        out = terms[0].astype(F32)
        for one in terms[1:]:
            out = out + one.astype(F32)
        return out.astype(BF)

    def sum_g(g, j, *more):
        return sum_of(own_g[g % OWN, c, j], p_g[g, j], *more)

    def sum_d(g, k, *more):
        return sum_of(own_d[g % OWN, c, k], p_d[g, k], *more)

    def dest_of(g, k):
        return down_piece(g % NL, c, k)[0]

    def next_moments(g, kind):
        st_do(g, kind, 1, "start")

        @pl.when(g + 1 < NG)
        def _():
            @pl.when(g >= 1)
            def _():
                st_do(g - 1, kind, 1, "wait")
            st_do(g + 1, kind, 0, "start")

    def final_g(g, rz):
        slot = g % 2
        st_do(g, "g", 0, "wait")
        if rz == 1:
            wait_rg(g, z)
            wait_rg(g, 4)
            total = sum_g(g, z, nwg[g, c, z], x_g[g])
        else:
            @pl.when(z == 0)
            def _():
                wait_rg(g, 4)
                nwg[g, c, z] = x_g[g]

            @pl.when(z == 3)
            def _():
                wait_rg(g, z)

            total = sum_g(g, z, nwg[g, c, z])
        for j in range(4):
            rows, cols = slice(80 * (j // 2), 80 * (j // 2) + 80), slice(S * (j % 2), S * (j % 2) + S)
            new, m, v = adamw(st_wg[slot, j].astype(F32), st_mg[slot, j], st_vg[slot, j], total[rows, cols].astype(F32))
            nwg[g, c, z, rows, cols] = new
            st_mg[slot, j] = m
            st_vg[slot, j] = v
        if rz == 1:
            ag_start_g(g, z, 1)
            ag_start_g(g, z, -1)
        else:
            ag_start_g(g, z, jnp.where(z == 0, 1, -1))
        partner_start_g(g, z)
        next_moments(g, "g")

    def final_d(g, rz):
        slot = g % 2
        st_do(g, "d", 0, "wait")
        for k in range(2):
            @pl.when(dest_of(g, k) == z)
            def _():
                if rz == 1:
                    wait_rd(g, k, 0)
                    wait_rd(g, k, 1)
                    total = sum_d(g, k, nwd[g, c, k], x_d[g // 2, k])
                else:
                    @pl.when(z == 0)
                    def _():
                        wait_rd(g, k, 1)
                        nwd[g, c, k] = x_d[g // 2, k]

                    @pl.when(z == 3)
                    def _():
                        wait_rd(g, k, 0)

                    total = sum_d(g, k, nwd[g, c, k])
                new, m, v = adamw(st_wd[slot, k].astype(F32), st_md[slot, k], st_vd[slot, k], total.astype(F32))
                nwd[g, c, k] = new
                st_md[slot, k] = m
                st_vd[slot, k] = v
                if rz == 1:
                    ag_start_d(g, k, 1)
                    ag_start_d(g, k, -1)
                else:
                    ag_start_d(g, k, jnp.where(z == 0, 1, -1))
                partner_start_d(g, k)

        next_moments(g, "d")

    def mirrored(rz, rd):
        plain = z == rz
        return plain | (z == 3 - rz), jnp.where(plain, rd, 3 - rd), jnp.where(plain, 1, -1), jnp.where(plain, 0, 1)

    def reduce_step(g, kind, rz, rd):
        active, d, dz, side = mirrored(rz, rd)
        if kind == "g":
            @pl.when(active)
            def _():
                if rz == 0:
                    p_g[g, d] = sum_g(g, d)
                else:
                    wait_rg(g, d)
                    p_g[g, d] = sum_g(g, d, nwg[g, c, d])
                rs_start_g(g, d, dz)
            return
        for k in range(2):
            @pl.when(active & (dest_of(g, k) == d))
            def _():
                if rz == 0:
                    p_d[g, k] = sum_d(g, k)
                else:
                    wait_rd(g, k, side)
                    p_d[g, k] = sum_d(g, k, nwd[g, c, k])
                rs_start_d(g, k, d, dz)

    def final_step(g, kind, rz):
        final = final_g if kind == "g" else final_d
        pl.when((z == rz) | (z == 3 - rz))(lambda: final(g, rz))

    def gather_step(g, kind, rz, rd):
        active, d, dz, _ = mirrored(rz, rd)
        if kind == "g":
            @pl.when(active)
            def _():
                wait_ag(g, d)
                if rz < 3:
                    ag_start_g(g, d, dz)
                partner_start_g(g, d)
            return
        for k in range(2):
            @pl.when(active & (dest_of(g, k) == d))
            def _():
                wait_ad(g, k)
                if rz < 3:
                    ag_start_d(g, k, dz)
                partner_start_d(g, k)

    def partner_step(g, kind, rz):
        one = own_copies(g)["gd".index(kind)]
        pl.when((z == rz) | (z == 3 - rz))(lambda: one().wait_recv())

    def own_sent(g):
        for one in own_copies(g):
            one().wait_send()

    steps = {"partner": partner_step, "sum": reduce_step, "final": final_step, "gather": gather_step, "sent": own_sent}

    def tick(it, s):
        todo = [((FIRST + o) // PARTS, n, step) for n, (*step, o) in enumerate(SCHEDULE) if (FIRST + o) % PARTS == s]
        for lag, _, (name, *rest) in sorted(todo, key=lambda one: (-one[0], one[1])):
            when_chunk(it - lag, functools.partial(lambda g, name, rest: steps[name](g, *rest), name=name, rest=rest))

    def when_chunk(g, fn):
        pl.when((g >= 0) & (g < NG))(lambda: fn(g))

    ROWS = 256
    NT = T // ROWS

    def tile_of(i):
        return pl.ds(pl.multiple_of(i * ROWS, ROWS), ROWS)

    def tile_in(src, i):
        return pltpu.make_async_copy(src.at[tile_of(i)], A.at[tile_of(i)], sem_in.at[i])

    def tiles_in(src):
        @pl.loop(0, NT)
        def _(i):
            tile_in(src, i).start()

    y_in = pltpu.make_async_copy(dy_h, Y, sem_in.at[NT])
    tiles_in(x_h)
    w_start(0)
    w_start(1)
    y_in.start()
    st_do(0, "g", 0, "start")
    st_do(0, "d", 0, "start")

    @pl.loop(0, NT)
    def _(i):
        tile_in(x_h, i).wait()
        rows = tile_of(i)
        wide, scale = norm_of(A[rows, :])
        A[rows, :] = (wide * scale).astype(BF)
        ACC[rows, :] = jnp.zeros((ROWS, D), F32)

    y_in.wait()
    a_out = pltpu.make_async_copy(A, a0_h, sem_in.at[NT])
    at_out = pltpu.make_async_copy(AT, a0t_h, sem_in.at[NT + 1])
    a_out.start()

    def forward(n):
        for t in range(T // TILE):
            rows = pl.ds(t * TILE, TILE)
            a = A[rows, :]
            total = ACC[rows, :]
            for slot in ((2 * n) % WS, (2 * n + 1) % WS):
                both = dot(a, WGU[slot])
                gate, up = both[:, :C], both[:, C:]
                hid = (gate * jax.nn.sigmoid(gate) * up).astype(BF)
                total = total + dot(hid, WD[slot])
            ACC[rows, :] = total

    @pl.loop(0, NL // 2)
    def _(n):
        w_wait(2 * n)
        w_wait(2 * n + 1)
        w_start(2 * n + 2)
        w_start(2 * n + 3)
        forward(n)

        @pl.when(n < T // TILE)
        def _():
            rows = pl.ds(pl.multiple_of(n * TILE, TILE), TILE)
            AT[:, rows] = A[rows, :].T
            YT[:, rows] = Y[rows, :].T

    at_out.start()
    a_out.wait()
    tiles_in(x_h)
    at_out.wait()

    def h1_out(i):
        return pltpu.make_async_copy(HS.at[i % 2], h1_h.at[tile_of(i)], sem_hs.at[i % 2])

    @pl.loop(0, NT)
    def _(i):
        pl.when(i >= 2)(lambda: h1_out(i - 2).wait())
        tile_in(x_h, i).wait()
        rows = tile_of(i)
        h = (A[rows, :].astype(F32) + ACC[rows, :].astype(BF).astype(F32)).astype(BF)
        HS[i % 2] = h
        h1_out(i).start()
        wide, scale = norm_of(h)
        a = (wide * scale).astype(BF)
        A[rows, :] = a
        AT[:, rows] = a.T
        ACC[rows, :] = jnp.zeros((ROWS, D), F32)

    h1_out(NT - 2).wait()
    h1_out(NT - 1).wait()
    pl.semaphore_wait(barrier, 1 + jnp.where(z > 0, 1, 0) + jnp.where(z < 3, 1, 0))

    at_in = pltpu.make_async_copy(a0t_h, AT, sem_in.at[NT])

    def between_layers():
        @pl.loop(0, NT)
        def _(i):
            tile_in(h1_h, i).wait()
            rows = tile_of(i)
            wide, scale = norm_of(A[rows, :])
            ct = ACC[rows, :].astype(BF).astype(F32)
            by_scale = jnp.sum(ct * wide, -1, keepdims=True)
            by_h = ct * scale - wide * (by_scale * scale * scale * scale * (1.0 / D))
            y = (Y[rows, :].astype(F32) + by_h.astype(BF).astype(F32)).astype(BF)
            Y[rows, :] = y
            YT[:, rows] = y.T
            tile_in(a0_h, i).start()

        @pl.loop(0, NT)
        def _(i):
            tile_in(a0_h, i).wait()

        at_in.wait()

    def tiles(g, first, last):
        slot = (g + NL) % WS
        for t in range(first, last):
            rows = pl.ds(t * TILE, TILE)
            both = dot(A[rows, :], WGU[slot])
            gate, up = both[:, :C], both[:, C:]
            by_hid = dot_t(Y[rows, :], WD[slot]).astype(BF).astype(F32)
            sig = jax.nn.sigmoid(gate)
            silu = gate * sig
            HID[rows, :] = (silu * up).astype(BF)
            DGU[rows, C:] = (by_hid * silu).astype(BF)
            DGU[rows, :C] = (by_hid * up * (sig + silu * (1.0 - sig))).astype(BF)

    def input_grad(g):
        slot = (g + NL) % WS
        for t in range(T // TILE):
            rows = pl.ds(t * TILE, TILE)
            ACC[rows, :] += dot_t(DGU[rows, :], WGU[slot])

    def weight_grads(g):
        slot = g % OWN
        out = dot(AT[...], DGU[...]).astype(BF)
        for q in range(2):
            for b in range(8):
                own_g[slot, b % 2, b // 2, 80 * q : 80 * q + 80, :] = out[80 * b : 80 * b + 80, C * q : C * q + C]

    def down_grad(g):
        slot = g % OWN
        out = dot(YT[...], HID[...]).T.astype(BF)
        mid = (g % NL) // 2 == 2
        for strip in range(2):
            for half in range(2):
                core = jnp.where(mid, half, strip)
                k = jnp.where(mid, strip, half)
                row = S * strip + 64 * half
                own_d[slot, core, k] = out[row : row + 64, :]

    def part(g, s):
        if s == 0:
            w_wait(g + NL)
            pl.when(g + 2 < NG)(lambda: w_start(g + NL + 2))
            pl.when(g == NL)(between_layers)
            tiles(g, 0, 2)
        elif s == 1:
            tiles(g, 2, 4)
            pl.when(g == NL - 1)(lambda: tiles_in(h1_h))
        elif s == 2:
            weight_grads(g)
            own_copies(g)[0]().start()
            pl.when(g == NL - 1)(at_in.start)
        elif s == 3:
            down_grad(g)
            own_copies(g)[1]().start()
        else:
            pl.when(g < NL)(lambda: input_grad(g))

    @pl.loop(0, NG + LAST)
    def _(g):
        for s in range(PARTS):
            pl.when(g < NG)(functools.partial(part, g, s))
            tick(g, s)

    for kind in "gd":
        st_do(NG - 2, kind, 1, "wait")
        st_do(NG - 1, kind, 1, "wait")

    def all_of(ref, send, recv):
        return remote(ref, ref, send, recv, to(0, True))

    all_of(nwg.at[:, 1 - c], sem_send.at[6], sem_pa.at[0]).wait_recv()
    all_of(nwd.at[:, 1 - c], sem_send.at[7], sem_pa.at[1]).wait_recv()

    def sent(which, ref):
        all_of(ref, sem_send.at[which], sem_pa.at[0]).wait_send()

    sent(0, nwg.at[:, 0, pl.ds(0, 3)])
    sent(1, p_d.at[pl.ds(0, 15)])
    sent(6, nwg.at[:, c])
    sent(7, nwd.at[:, c])

    for zz in range(4):
        right, left = ((1, 0), (2, 3), (3, 2), (0, 1))[zz]

        @pl.when(z == zz)
        def _():
            if right:
                sent(2, nwg.at[:, 0, pl.ds(0, right)])
                sent(4, p_d.at[pl.ds(0, 5 * right)])
            if left:
                sent(3, nwg.at[:, 0, pl.ds(0, left)])
                sent(5, p_d.at[pl.ds(0, 5 * left)])


def train(x, dy, *arrays):
    anyspace = pl.BlockSpec(memory_space=pl.ANY)
    sds = jax.ShapeDtypeStruct
    dma = pltpu.SemaphoreType.DMA
    vm = pltpu.VMEM
    outs = (
        vm((NG, 2, 4, 160, C), BF), vm((NG, 2, 2, 64, D), BF),
        sds((2, 80, FF), F32), sds((2, 80, FF), F32), sds((2, 320, D), F32),
        sds((2, 80, FF), F32), sds((2, 80, FF), F32), sds((2, 320, D), F32),
        sds((T, D), BF), sds((D, T), BF), sds((T, D), BF),
    )
    return pl.pallas_call(
        kernel,
        out_shape=outs,
        in_specs=[anyspace] * 11,
        out_specs=(pl.BlockSpec(memory_space=pltpu.VMEM),) * 2 + (anyspace,) * 9,
        scratch_shapes=[
            vm((2, 256, D), BF), vm((T, D), BF), vm((D, T), BF), vm((T, D), BF), vm((D, T), BF), vm((T, D), F32),
            vm((T, C), BF), vm((T, 2 * C), BF), vm((WS, D, 2 * C), BF), vm((WS, C, D), BF),
            vm((OWN, 2, 4, 160, C), BF), vm((OWN, 2, 2, 64, D), BF),
            vm((NG, 4, 160, C), BF), vm((NG, 2, 64, D), BF), vm((NG, 160, C), BF), vm((NG // 2, 2, 64, D), BF),
            vm((2, 4, 80, S), F32), vm((2, 4, 80, S), F32), vm((2, 4, 80, S), BF),
            vm((2, 2, 64, D), F32), vm((2, 2, 64, D), F32), vm((2, 2, 64, D), BF),
            dma((10,)), dma((WS, 6)), dma((2, 3, 6)), dma((2, 2, 6)), dma((8,)), dma((2,)), dma((OWN, 2)), dma((NG,)), dma((NG,)),
            dma((NG, 5)), dma((NG, 2, 2)), dma((NG, 4)), dma((NG, 2)), dma((2,)),
        ],
        compiler_params=pltpu.CompilerParams(
            collective_id=0, has_side_effects=True, vmem_limit_bytes=47000000),
        name="train",
    )(x, dy, *arrays)


def place(nwg, nwd, *refs):
    moments, (wg, wu, wd), outs, (buf_mg, buf_md, sem_out, sem_m, sem_mo) = refs[:6], refs[6:9], refs[9:15], refs[15:]

    def moment(j):
        buf = buf_md.at[j // 3] if j % 3 == 2 else buf_mg.at[2 * (j // 3) + j % 3]
        return (
            functools.partial(pltpu.make_async_copy, moments[j], buf, sem_m.at[j]),
            functools.partial(pltpu.make_async_copy, buf, outs[j], sem_mo.at[j]),
        )

    def store(g, act):
        layer, i = 1 - g // NL, g % NL
        f = strips_of(i)

        @pl.loop(0, 8)
        def _(b):
            rows = pl.ds(pl.multiple_of(80 * b, 80), 80)
            for q, out in enumerate((wg, wu)):
                for k in range(2):
                    src = nwg.at[g, b % 2, b // 2, pl.ds(80 * q, 80), pl.ds(S * k, S)]
                    getattr(pltpu.make_async_copy(src, out.at[layer, rows, pl.ds(f[k], S)], sem_out.at[0]), act)()

        for core in range(2):
            for k in range(2):
                dest, off = down_piece(i, core, k)
                rows = pl.ds(pl.multiple_of(640 * dest + 320 * core + off, 64), 64)
                getattr(pltpu.make_async_copy(nwd.at[g, core, k], wd.at[layer, rows], sem_out.at[1]), act)()

    for j in range(6):
        moment(j)[0]().start()

    @pl.loop(0, NG)
    def _(g):
        store(g, "start")

    for j in range(6):
        moment(j)[0]().wait()
        moment(j)[1]().start()

    for j in range(6):
        moment(j)[1]().wait()

    @pl.loop(0, NG)
    def _(g):
        store(g, "wait")


def finish(*arrays):
    anyspace = pl.BlockSpec(memory_space=pl.ANY)
    sds = jax.ShapeDtypeStruct
    dma = pltpu.SemaphoreType.DMA
    moments = [sds(one.shape, one.dtype) for one in arrays[2:]]
    return pl.pallas_call(
        place,
        out_shape=(sds((2, D, FF), BF), sds((2, D, FF), BF), sds((2, FF, D), BF), *moments),
        in_specs=[pl.BlockSpec(memory_space=pltpu.VMEM)] * 2 + [pl.BlockSpec(memory_space=pltpu.HBM)] * 6,
        out_specs=(anyspace,) * 9,
        scratch_shapes=[
            pltpu.VMEM((4, 2, 80, FF), F32), pltpu.VMEM((2, 2, 320, D), F32),
            dma((2,)), dma((6,)), dma((6,)),
        ],
        compiler_params=pltpu.CompilerParams(vmem_limit_bytes=20000000),
        name="place",
    )(*(pltpu.with_memory_space_constraint(one, pltpu.VMEM if n < 2 else pltpu.HBM) for n, one in enumerate(arrays)))


def solution(mesh):
    def step(x, dy, *arrays):
        return finish(*train(x[0], dy[0], *arrays)[:8])

    whole = P(None, None, None)
    rows = P(None, "dp", None)
    seq = P(("rep", "dp"), None, None)
    return jax.shard_map(
        step,
        mesh=mesh,
        in_specs=(seq, seq) + (whole,) * 3 + (rows,) * 6,
        out_specs=(P("rep", None, None),) * 3 + (P("rep", "dp", None),) * 6,
        check_vma=False,
    )
```

time: 663 us -> 301 us (0.45); the launches traced: 655 us -> 301 us
  waiting for transfers between devices: 324 us -> 0 us
  Pallas kernels: 0 us -> 300 us
  matrix products: 246 us -> 0 us
  other arithmetic: 45.9 us -> 0 us
  local copies, waits for them, and re-layouts: 23 us -> 0 us
  between operations: 14.9 us -> 0.81 us
    pallas_call x0 -> x2, Pallas kernels: none -> 300 us  [the longest x1 287 us: train(): pl.pallas_call(kernel, out_shape=outs, in_specs=[anyspace] * 11, out_spec...]
    dot_general x15 -> x0, matrix products: 246 us -> none  [the longest x5 92.9 us: layer(): gate = jnp.dot(a, w['w_gate'], preferred_element_type=jnp.float32)]
    all_gather x6 -> x0, waiting for transfers between devices: 212 us -> none  [step(): new[k, number] = (lax.all_gather(one, 'dp', axis=0, tiled=True), m1, v1)]
    reduce_scatter x6 -> x0, waiting for transfers between devices: 110 us -> none  [step(): g = lax.psum_scatter(by_w[NAMES[k]], 'dp', scatter_dimension=0, tiled=True)]
    another operation x6 -> x0, other arithmetic: 27.1 us -> none  [step(): jnp.stack([new[k, number][which] for number in range(layers)])]
    slice x3 -> x0, local copies, waits for them, and re-layouts: 15.4 us -> none  [the longest x2 10.3 us: step(): w[number]]
    convert_element_type x3 -> x0, other arithmetic: 14 us -> none  [adamw(): return ((w - 0.02 * step).astype(jnp.bfloat16), m, v)]
    unnamed x44 -> x0, local copies, waits for them, and re-layouts: 7.58 us -> none
  transfers between devices with their start and end apart: 12 -> 0, of which waited for: 9 -> 0; matrix products, arithmetic and copies ran while one was open for 27% -> 0% of each run, Pallas kernels for 0% -> 0%
where the time goes in v3:
time: 301 us
  Pallas kernels  300 us (100%)
    pallas_call x1, Pallas kernels, train(): pl.pallas_call(kernel, out_shape=outs, in_specs=[anyspace] * 11, out_spec...  287 us
    pallas_call x1, Pallas kernels, finish(): pl.pallas_call(place, out_shape=(sds((2, D, FF), BF), sds((2, D, FF), BF)...  13.3 us

profile of v3, /device:TPU:0, one launch (start us, length us, event | category | flops | bytes accessed | tf_op | source)
XLA Modules:
  0.0 301.1 jit_solution(17871439549370564987)
XLA Ops:
  0.6 287.0 %train.1 = (bf16[20,2,4,160,256]{4,3,2,1,0:T(8,128)(2,1)S(1)}, bf16[20,2,2,64,640]{4,3,2,1,0:T(8,128)(2,1)S(1)}, f32[2,80,2560]{2,1,0:T(8,128)}, f32[2,80,2560]{...) custom-call(bf16[2048,640]{1,0:T(8,128)(2,1)} %bitcast.2, ...), custom_call_target="tpu_custom_call" | custom-call | tf_op jit(solution)/shard_map/train/pallas_call | solution.py:603
  287.6 13.3 %place.1 = (bf16[2,640,2560]{2,1,0:T(8,128)(2,1)}, bf16[2,640,2560]{2,1,0:T(8,128)(2,1)}, bf16[2,2560,640]{2,1,0:T(8,128)(2,1)}, f32[2,80,2560]{2,1,0:T(8,128)},...) custom-call(bf16[20,2,4,160,256]{4,3,2,1,0:T(8,128)(2,1)S(1)} %get-t, ...), custom_call_target="tpu_custom_call" | custom-call | tf_op jit(solution)/shard_map/place/pallas_call | solution.py:676

commit v4 on v3

v4 whole, which is shorter than its diff:
```python
import functools

import jax
import jax.numpy as jnp
from jax import lax
from jax.experimental import pallas as pl
from jax.experimental.pallas import tpu as pltpu
from jax.sharding import PartitionSpec as P

MESH = pl.DeviceIdType.MESH
BF = jnp.bfloat16
F32 = jnp.float32
T, D, FF = 2048, 640, 2560
C = 256
S = 128
NL = 10
NG = 20
TILE = 512
EPS = 1e-6
WS = 4
OWN = 3
KEEP = 4
RING = 8
PARTS = 5
FIRST = 2
SCHEDULE = (
    ("partner", "g", 0, 2), ("partner", "d", 0, 1), ("partner", "g", 1, 5), ("partner", "d", 1, 7),
    ("sum", "g", 0, 3, 2), ("sum", "d", 0, 3, 3), ("sum", "g", 0, 2, 2), ("sum", "d", 0, 2, 1), ("sum", "g", 0, 1, 6), ("sum", "d", 0, 1, 3),
    ("sum", "g", 1, 3, 5), ("sum", "d", 1, 3, 9), ("sum", "g", 1, 2, 6), ("sum", "d", 1, 2, 7), ("sum", "g", 2, 3, 9), ("sum", "d", 2, 3, 11),
    ("final", "g", 1, 9), ("final", "d", 1, 11), ("final", "g", 0, 14), ("final", "d", 0, 15), ("sent", 12), ("sums_sent", 18),
    ("gather", "g", 2, 1, 12), ("gather", "d", 2, 1, 13), ("gather", "g", 1, 0, 17), ("gather", "d", 1, 0, 17),
    ("gather", "g", 3, 1, 19), ("gather", "d", 3, 1, 23), ("gather", "g", 2, 0, 20), ("gather", "d", 2, 0, 21),
    ("gather", "g", 3, 0, 26), ("gather", "d", 3, 0, 25), ("gather", "g", 3, 2, 21), ("gather", "d", 3, 2, 17),
)
LAST = max((FIRST + one[-1]) // PARTS for one in SCHEDULE)


def chunk_of(i):
    pair, t = i % 2, i // 2
    low = t <= 2
    z1, s1 = jnp.where(low, pair, 3 - pair), jnp.where(low, t, 4 - t)
    z2, s2 = jnp.where(low, 3 - pair, pair), jnp.where(low, 4 - t, t)
    return t, z1, s1, z2, s2


def strips_of(i):
    _, z1, s1, z2, s2 = chunk_of(i)
    return pl.multiple_of(640 * z1 + S * s1, S), pl.multiple_of(640 * z2 + S * s2, S)


def down_piece(i, c, k):
    t, z1, s1, z2, s2 = chunk_of(i)
    mid = t == 2
    dest = jnp.where(mid, z1 if k == 0 else z2, jnp.where(c == 0, z1, z2))
    s = jnp.where(c == 0, s1, s2)
    off = jnp.where(mid, jnp.where(c == 0, 256, 0), 64 * (2 * s + k - 5 * c))
    return dest, pl.multiple_of(off, 64)


def norm_of(h):
    wide = h.astype(F32)
    scale = lax.rsqrt(jnp.mean(wide * wide, -1, keepdims=True) + EPS)
    return wide, scale


def dot(a, b):
    return jnp.dot(a, b, preferred_element_type=F32)


def dot_t(a, b):
    return lax.dot_general(a, b, (((1,), (1,)), ((), ())), preferred_element_type=F32)


def adamw(w, m, v, g):
    m = 0.9 * m + 0.1 * g
    v = 0.95 * v + 0.05 * g * g
    step = m * lax.rsqrt(v + 1e-8) + 0.1 * w
    return (w - 0.02 * step).astype(BF), m, v


def kernel(
    x_h, dy_h, wg_h, wu_h, wd_h, mg_h, mu_h, md_h, vg_h, vu_h, vd_h,
    nwg, nwd, omg, omu, omd, ovg, ovu, ovd, a0_h, h1_h,
    A, AT, Y, YT, ACC, HID, DGU, WGU, WD, own_g, own_d, p_g, p_d, x_g, x_d,
    st_wg, st_wd,
    sem_in, sem_w, sem_ld, sem_send, sem_rs, sem_h, sem_own, sem_pg, sem_pd, sem_rg, sem_rd, sem_ag, sem_ad, sem_pa,
):
    rep, dp = lax.axis_index("rep"), lax.axis_index("dp")
    z, c = dp // 2, dp % 2
    is_end = (z == 0) | (z == 3)
    is_mid = (z == 1) | (z == 2)

    def to(dz, flip=False):
        return (rep, (z + dz) * 2 + ((1 - c) if flip else c))

    barrier = pltpu.get_barrier_semaphore()
    pl.semaphore_signal(barrier, inc=1, device_id=to(0, True), device_id_type=MESH)

    @pl.when(z > 0)
    def _():
        pl.semaphore_signal(barrier, inc=1, device_id=to(-1), device_id_type=MESH)

    @pl.when(z < 3)
    def _():
        pl.semaphore_signal(barrier, inc=1, device_id=to(1), device_id_type=MESH)

    def w_copies(n):
        layer = jnp.where((n >= 10) & (n < 20), 1, 0)
        slot = n % WS
        out = []
        for k, f in enumerate(strips_of(n % NL)):
            out.append(functools.partial(pltpu.make_async_copy, wg_h.at[layer, :, pl.ds(f, S)], WGU.at[slot, :, pl.ds(S * k, S)], sem_w.at[slot, k]))
            out.append(functools.partial(pltpu.make_async_copy, wu_h.at[layer, :, pl.ds(f, S)], WGU.at[slot, :, pl.ds(C + S * k, S)], sem_w.at[slot, 2 + k]))
            out.append(functools.partial(pltpu.make_async_copy, wd_h.at[layer, pl.ds(f, S), :], WD.at[slot, pl.ds(S * k, S), :], sem_w.at[slot, 4 + k]))
        return out

    def w_start(n):
        for one in w_copies(n):
            one().start()

    def w_wait(n):
        for one in w_copies(n):
            one().wait()

    def moments_in():
        return [functools.partial(pltpu.make_async_copy, src, dst, sem_ld.at[n])
                for n, (src, dst) in enumerate(((mg_h, omg), (mu_h, omu), (md_h, omd), (vg_h, ovg), (vu_h, ovu), (vd_h, ovd)))]

    def keep_weights(g):
        slot, w = g % KEEP, (g + NL) % WS
        st_wg[slot] = WGU[w, pl.ds(pl.multiple_of(80 * dp, 16), 80), :]
        mid = (g % NL) // 2 == 2
        for k in range(2):
            @pl.when(dest_of(g, k) == z)
            def _():
                row = jnp.where(mid, S * k + 64 * c, S * c + 64 * k)
                st_wd[slot, k] = WD[w, pl.ds(pl.multiple_of(row, 64), 64), :]

    def remote(src, dst, send, recv, where):
        return pltpu.make_async_remote_copy(src, dst, send, recv, device_id=where, device_id_type=MESH)

    def rs_start_g(g, j, dz):
        to_end = (dz == -1) & (j == z - 1)

        @pl.when(to_end)
        def _():
            remote(p_g.at[g % RING, j], x_g.at[g % RING], sem_rs.at[g % RING, j], sem_rg.at[g, 4], to(-1)).start()

        @pl.when(jnp.logical_not(to_end))
        def _():
            remote(p_g.at[g % RING, j], nwg.at[g, c, j], sem_rs.at[g % RING, j], sem_rg.at[g, j], to(dz)).start()

    def rs_start_d(g, k, d, dz):
        to_end = (dz == -1) & (d == z - 1)

        @pl.when(to_end)
        def _():
            remote(p_d.at[g % RING, k], x_d.at[g // 2 % (RING // 2), k], sem_rs.at[g % RING, 4 + k], sem_rd.at[g, k, 1], to(-1)).start()

        @pl.when(jnp.logical_not(to_end))
        def _():
            side = jnp.where(dz == 1, 0, 1)
            remote(p_d.at[g % RING, k], nwd.at[g, c, k], sem_rs.at[g % RING, 4 + k], sem_rd.at[g, k, side], to(dz)).start()

    def wait_rg(g, slot):
        remote(p_g.at[g % RING, 0], x_g.at[g % RING], sem_send.at[0], sem_rg.at[g, slot], to(0, True)).wait_recv()

    def wait_rd(g, k, side):
        remote(p_d.at[g % RING, k], x_d.at[g // 2 % (RING // 2), k], sem_send.at[1], sem_rd.at[g, k, side], to(0, True)).wait_recv()

    def ag_start_g(g, d, dz):
        here = nwg.at[g, c, d]
        remote(here, here, sem_send.at[jnp.where(dz == 1, 2, 3)], sem_ag.at[g, d], to(dz)).start()

    def ag_start_d(g, k, dz):
        here = nwd.at[g, c, k]
        remote(here, here, sem_send.at[jnp.where(dz == 1, 4, 5)], sem_ad.at[g, k], to(dz)).start()

    def partner_start_g(g, d):
        here = nwg.at[g, c, d]
        remote(here, here, sem_send.at[6], sem_pa.at[0], to(0, True)).start()

    def partner_start_d(g, k):
        here = nwd.at[g, c, k]
        remote(here, here, sem_send.at[7], sem_pa.at[1], to(0, True)).start()

    def wait_ag(g, d):
        here = nwg.at[g, c, d]
        remote(here, here, sem_send.at[2], sem_ag.at[g, d], to(0, True)).wait_recv()

    def wait_ad(g, k):
        here = nwd.at[g, c, k]
        remote(here, here, sem_send.at[4], sem_ad.at[g, k], to(0, True)).wait_recv()

    def own_copies(g):
        slot = g % OWN
        return (
            functools.partial(pltpu.make_async_remote_copy,
                own_g.at[slot, 1 - c], p_g.at[g % RING], sem_own.at[slot, 0], sem_pg.at[g], device_id=to(0, True), device_id_type=MESH),
            functools.partial(pltpu.make_async_remote_copy,
                own_d.at[slot, 1 - c], p_d.at[g % RING], sem_own.at[slot, 1], sem_pd.at[g], device_id=to(0, True), device_id_type=MESH),
        )

    def sum_of(*terms):
        out = terms[0].astype(F32)
        for one in terms[1:]:
            out = out + one.astype(F32)
        return out.astype(BF)

    def sum_g(g, j, *more):
        return sum_of(own_g[g % OWN, c, j], p_g[g % RING, j], *more)

    def sum_d(g, k, *more):
        return sum_of(own_d[g % OWN, c, k], p_d[g % RING, k], *more)

    def dest_of(g, k):
        return down_piece(g % NL, c, k)[0]

    def final_g(g, rz):
        slot, layer, f = g % KEEP, 1 - g // NL, strips_of(g % NL)
        if rz == 1:
            wait_rg(g, z)
            wait_rg(g, 4)
            total = sum_g(g, z, nwg[g, c, z], x_g[g % RING])
        else:
            @pl.when(z == 0)
            def _():
                wait_rg(g, 4)
                nwg[g, c, z] = x_g[g % RING]

            @pl.when(z == 3)
            def _():
                wait_rg(g, z)

            total = sum_g(g, z, nwg[g, c, z])
        for j in range(4):
            q, k = j // 2, j % 2
            rows, cols, at = slice(80 * q, 80 * q + 80), slice(S * k, S * k + S), pl.ds(f[k], S)
            om, ov = ((omg, ovg), (omu, ovu))[q]
            w = st_wg[slot, :, C * q + S * k : C * q + S * k + S].astype(F32)
            new, m, v = adamw(w, om[layer, :, at], ov[layer, :, at], total[rows, cols].astype(F32))
            nwg[g, c, z, rows, cols] = new
            om[layer, :, at] = m
            ov[layer, :, at] = v
        if rz == 1:
            ag_start_g(g, z, 1)
            ag_start_g(g, z, -1)
        else:
            ag_start_g(g, z, jnp.where(z == 0, 1, -1))
        partner_start_g(g, z)

    def final_d(g, rz):
        slot, layer = g % KEEP, 1 - g // NL
        for k in range(2):
            @pl.when(dest_of(g, k) == z)
            def _():
                if rz == 1:
                    wait_rd(g, k, 0)
                    wait_rd(g, k, 1)
                    total = sum_d(g, k, nwd[g, c, k], x_d[g // 2 % (RING // 2), k])
                else:
                    @pl.when(z == 0)
                    def _():
                        wait_rd(g, k, 1)
                        nwd[g, c, k] = x_d[g // 2 % (RING // 2), k]

                    @pl.when(z == 3)
                    def _():
                        wait_rd(g, k, 0)

                    total = sum_d(g, k, nwd[g, c, k])
                at = pl.ds(down_piece(g % NL, c, k)[1], 64)
                new, m, v = adamw(st_wd[slot, k].astype(F32), omd[layer, at, :], ovd[layer, at, :], total.astype(F32))
                nwd[g, c, k] = new
                omd[layer, at, :] = m
                ovd[layer, at, :] = v
                if rz == 1:
                    ag_start_d(g, k, 1)
                    ag_start_d(g, k, -1)
                else:
                    ag_start_d(g, k, jnp.where(z == 0, 1, -1))
                partner_start_d(g, k)

    def mirrored(rz, rd):
        plain = z == rz
        return plain | (z == 3 - rz), jnp.where(plain, rd, 3 - rd), jnp.where(plain, 1, -1), jnp.where(plain, 0, 1)

    def reduce_step(g, kind, rz, rd):
        active, d, dz, side = mirrored(rz, rd)
        if kind == "g":
            @pl.when(active)
            def _():
                if rz == 0:
                    p_g[g % RING, d] = sum_g(g, d)
                else:
                    wait_rg(g, d)
                    p_g[g % RING, d] = sum_g(g, d, nwg[g, c, d])
                rs_start_g(g, d, dz)
            return
        for k in range(2):
            @pl.when(active & (dest_of(g, k) == d))
            def _():
                if rz == 0:
                    p_d[g % RING, k] = sum_d(g, k)
                else:
                    wait_rd(g, k, side)
                    p_d[g % RING, k] = sum_d(g, k, nwd[g, c, k])
                rs_start_d(g, k, d, dz)

    def final_step(g, kind, rz):
        final = final_g if kind == "g" else final_d
        pl.when((z == rz) | (z == 3 - rz))(lambda: final(g, rz))

    def gather_step(g, kind, rz, rd):
        active, d, dz, _ = mirrored(rz, rd)
        if kind == "g":
            @pl.when(active)
            def _():
                wait_ag(g, d)
                if rz < 3:
                    ag_start_g(g, d, dz)
                partner_start_g(g, d)
            return
        for k in range(2):
            @pl.when(active & (dest_of(g, k) == d))
            def _():
                wait_ad(g, k)
                if rz < 3:
                    ag_start_d(g, k, dz)
                partner_start_d(g, k)

    def partner_step(g, kind, rz):
        one = own_copies(g)["gd".index(kind)]
        pl.when((z == rz) | (z == 3 - rz))(lambda: one().wait_recv())

    def sums_sent(g):
        slot = g % RING

        def wait(ref, at):
            remote(ref, ref, sem_rs.at[slot, at], sem_pa.at[0], to(0, True)).wait_send()

        for j in range(4):
            pl.when(z != j)(lambda j=j: wait(p_g.at[slot, j], j))
        for k in range(2):
            pl.when(dest_of(g, k) != z)(lambda k=k: wait(p_d.at[slot, k], 4 + k))

    def own_sent(g):
        for one in own_copies(g):
            one().wait_send()

    steps = {"partner": partner_step, "sum": reduce_step, "final": final_step, "gather": gather_step, "sent": own_sent, "sums_sent": sums_sent}

    def tick(it, s):
        todo = [((FIRST + o) // PARTS, n, step) for n, (*step, o) in enumerate(SCHEDULE) if (FIRST + o) % PARTS == s]
        for lag, _, (name, *rest) in sorted(todo, key=lambda one: (-one[0], one[1])):
            when_chunk(it - lag, functools.partial(lambda g, name, rest: steps[name](g, *rest), name=name, rest=rest))

    def when_chunk(g, fn):
        pl.when((g >= 0) & (g < NG))(lambda: fn(g))

    NT = T // TILE

    def tile_of(i):
        return pl.ds(pl.multiple_of(i * TILE, TILE), TILE)

    def tile_in(src, i):
        return pltpu.make_async_copy(src.at[tile_of(i)], A.at[tile_of(i)], sem_in.at[i])

    def tiles_in(src):
        @pl.loop(0, NT)
        def _(i):
            tile_in(src, i).start()

    def h_parts(i):
        rows = tile_of(i)
        return (DGU.at[rows], pl.ds(0, 512)), (HID.at[rows, pl.ds(0, 128)], pl.ds(512, 128))

    def x_again(i):
        return [functools.partial(pltpu.make_async_copy, x_h.at[tile_of(i), cols], ref, sem_h.at[0, i, k]) for k, (ref, cols) in enumerate(h_parts(i))]

    def h1_out(i):
        return [functools.partial(pltpu.make_async_copy, ref, h1_h.at[tile_of(i), cols], sem_h.at[1, i, k]) for k, (ref, cols) in enumerate(h_parts(i))]

    def each(copies, act):
        for one in copies:
            getattr(one(), act)()

    y_in = pltpu.make_async_copy(dy_h, Y, sem_in.at[NT + 1])
    tile_in(x_h, 0).start()
    w_start(0)
    w_start(1)
    for t in range(1, NT):
        tile_in(x_h, t).start()
    a_out = pltpu.make_async_copy(A, a0_h, sem_in.at[NT])

    def forward_tile(n, t):
        rows = pl.ds(t * TILE, TILE) if isinstance(t, int) else tile_of(t)
        a = A[rows, :]
        total = 0.0
        for slot in ((2 * n) % WS, (2 * n + 1) % WS):
            both = dot(a, WGU[slot])
            gate, up = both[:, :C], both[:, C:]
            hid = (gate * jax.nn.sigmoid(gate) * up).astype(BF)
            total = total + dot(hid, WD[slot])
        return rows, total

    def turn(src, dst):
        @pl.loop(0, NT)
        def _(t):
            rows = tile_of(t)
            dst[:, rows] = src[rows, :].T

    def forward_weights(n):
        w_wait(2 * n)
        w_wait(2 * n + 1)
        w_start(2 * n + 2)
        w_start(2 * n + 3)

    for t in range(NT):
        tile_in(x_h, t).wait()
        rows = pl.ds(t * TILE, TILE)
        wide, scale = norm_of(A[rows, :])
        A[rows, :] = (wide * scale).astype(BF)
        if t == 0:
            forward_weights(0)
        rows, total = forward_tile(0, t)
        ACC[rows, :] = total
    a_out.start()
    y_in.start()
    for t in range(NT):
        each(x_again(t), "start")
    each(moments_in(), "start")

    @pl.loop(1, NL // 2 - 1)
    def _(n):
        forward_weights(n)
        for t in range(NT):
            rows, total = forward_tile(n, t)
            ACC[rows, :] += total

    a_out.wait()
    forward_weights(NL // 2 - 1)
    for t in range(NT):
        each(x_again(t), "wait")
    def last_forward(t):
        rows, total = forward_tile(NL // 2 - 1, t)
        total = (ACC[rows, :] + total).astype(BF).astype(F32)
        ACC[rows, :] = jnp.zeros((TILE, D), F32)
        ha = (DGU[rows, :].astype(F32) + total[:, :512]).astype(BF)
        hb = (HID[rows, :128].astype(F32) + total[:, 512:]).astype(BF)
        DGU[rows, :] = ha
        HID[rows, :128] = hb
        ha, hb = ha.astype(F32), hb.astype(F32)
        mean = (jnp.sum(ha * ha, -1, keepdims=True) + jnp.sum(hb * hb, -1, keepdims=True)) * (1.0 / D)
        scale = lax.rsqrt(mean + EPS)
        A[rows, :512] = (ha * scale).astype(BF)
        A[rows, 512:] = (hb * scale).astype(BF)
        AT[:, rows] = A[rows, :].T
        each(h1_out(t), "start")

    @pl.loop(0, NT // 2)
    def _(i):
        last_forward(2 * i)
        last_forward(2 * i + 1)

    y_in.wait()
    turn(Y, YT)
    each(moments_in(), "wait")
    pl.semaphore_wait(barrier, 1 + jnp.where(z > 0, 1, 0) + jnp.where(z < 3, 1, 0))

    def tiles(g, first, last):
        slot = (g + NL) % WS
        for t in range(first, last):
            rows = pl.ds(t * TILE, TILE)
            both = dot(A[rows, :], WGU[slot])
            gate, up = both[:, :C], both[:, C:]
            by_hid = dot_t(Y[rows, :], WD[slot]).astype(BF).astype(F32)
            sig = jax.nn.sigmoid(gate)
            silu = gate * sig
            HID[rows, :] = (silu * up).astype(BF)
            DGU[rows, C:] = (by_hid * silu).astype(BF)
            DGU[rows, :C] = (by_hid * up * (sig + silu * (1.0 - sig))).astype(BF)

    def input_grad(g):
        slot = (g + NL) % WS
        for t in range(NT):
            rows = pl.ds(t * TILE, TILE)
            ACC[rows, :] += dot_t(DGU[rows, :], WGU[slot])

    def last_input_grad(g):
        slot = (g + NL) % WS
        for t in range(NT):
            tile_in(h1_h, t).wait()
        @pl.loop(0, NT)
        def _(t):
            rows = tile_of(t)
            ct = (ACC[rows, :] + dot_t(DGU[rows, :], WGU[slot])).astype(BF).astype(F32)
            wide, scale = norm_of(A[rows, :])
            by_scale = jnp.sum(ct * wide, -1, keepdims=True)
            by_h = ct * scale - wide * (by_scale * scale * scale * scale * (1.0 / D))
            y = (Y[rows, :].astype(F32) + by_h.astype(BF).astype(F32)).astype(BF)
            Y[rows, :] = y
            YT[:, rows] = y.T
        for t in range(NT):
            tile_in(a0_h, t).start()

    def weight_grads(g):
        slot = g % OWN
        out = dot(AT[...], DGU[...]).astype(BF)
        for q in range(2):
            for b in range(8):
                own_g[slot, b % 2, b // 2, 80 * q : 80 * q + 80, :] = out[80 * b : 80 * b + 80, C * q : C * q + C]

    def down_grad(g):
        slot = g % OWN
        out = dot(YT[...], HID[...]).T.astype(BF)
        mid = (g % NL) // 2 == 2
        for strip in range(2):
            for half in range(2):
                core = jnp.where(mid, half, strip)
                k = jnp.where(mid, strip, half)
                row = S * strip + 64 * half
                own_d[slot, core, k] = out[row : row + 64, :]

    def part(g, s):
        if s == 0:
            w_wait(g + NL)
            pl.when(g + 2 < NG)(lambda: w_start(g + NL + 2))

            @pl.when(g == 0)
            def _():
                for t in range(NT):
                    each(h1_out(t), "wait")

            @pl.when(g == NL)
            def _():
                for t in range(NT):
                    tile_in(a0_h, t).wait()
                turn(A, AT)

            keep_weights(g)
            tiles(g, 0, 2)
        elif s == 1:
            tiles(g, 2, 4)
            pl.when(g == NL - 1)(lambda: tiles_in(h1_h))
        elif s == 2:
            weight_grads(g)
            own_copies(g)[0]().start()
        elif s == 3:
            down_grad(g)
            own_copies(g)[1]().start()
        else:
            pl.when(g < NL - 1)(lambda: input_grad(g))
            pl.when(g == NL - 1)(lambda: last_input_grad(g))

    @pl.loop(0, NG + LAST)
    def _(g):
        for s in range(PARTS):
            pl.when(g < NG)(functools.partial(part, g, s))
            tick(g, s)

    def all_of(ref, send, recv):
        return remote(ref, ref, send, recv, to(0, True))

    all_of(nwg.at[:, 1 - c], sem_send.at[6], sem_pa.at[0]).wait_recv()
    all_of(nwd.at[:, 1 - c], sem_send.at[7], sem_pa.at[1]).wait_recv()

    def sent(which, ref):
        all_of(ref, sem_send.at[which], sem_pa.at[0]).wait_send()

    sent(6, nwg.at[:, c])
    sent(7, nwd.at[:, c])

    for zz in range(4):
        right, left = ((1, 0), (2, 3), (3, 2), (0, 1))[zz]

        @pl.when(z == zz)
        def _():
            if right:
                sent(2, nwg.at[:, 0, pl.ds(0, right)])
                sent(4, nwd.at[pl.ds(0, 5 * right), 0])
            if left:
                sent(3, nwg.at[:, 0, pl.ds(0, left)])
                sent(5, nwd.at[pl.ds(0, 5 * left), 0])


def train(x, dy, *arrays):
    anyspace = pl.BlockSpec(memory_space=pl.ANY)
    sds = jax.ShapeDtypeStruct
    dma = pltpu.SemaphoreType.DMA
    vm = pltpu.VMEM
    outs = (
        vm((NG, 2, 4, 160, C), BF), vm((NG, 2, 2, 64, D), BF),
        vm((2, 80, FF), F32), vm((2, 80, FF), F32), vm((2, 320, D), F32),
        vm((2, 80, FF), F32), vm((2, 80, FF), F32), vm((2, 320, D), F32),
        sds((T, D), BF), sds((T, D), BF),
    )
    return pl.pallas_call(
        kernel,
        out_shape=outs,
        in_specs=[anyspace] * 11,
        out_specs=(pl.BlockSpec(memory_space=pltpu.VMEM),) * 8 + (anyspace,) * 2,
        scratch_shapes=[
            vm((T, D), BF), vm((D, T), BF), vm((T, D), BF), vm((D, T), BF), vm((T, D), F32),
            vm((T, C), BF), vm((T, 2 * C), BF), vm((WS, D, 2 * C), BF), vm((WS, C, D), BF),
            vm((OWN, 2, 4, 160, C), BF), vm((OWN, 2, 2, 64, D), BF),
            vm((RING, 4, 160, C), BF), vm((RING, 2, 64, D), BF), vm((RING, 160, C), BF), vm((RING // 2, 2, 64, D), BF),
            vm((KEEP, 80, 2 * C), BF), vm((KEEP, 2, 64, D), BF),
            dma((10,)), dma((WS, 6)), dma((6,)), dma((8,)), dma((RING, 6)), dma((2, 4, 2)), dma((OWN, 2)), dma((NG,)), dma((NG,)),
            dma((NG, 5)), dma((NG, 2, 2)), dma((NG, 4)), dma((NG, 2)), dma((2,)),
        ],
        compiler_params=pltpu.CompilerParams(
            collective_id=0, has_side_effects=True, vmem_limit_bytes=37000000),
        name="train",
    )(x, dy, *arrays)


def place(nwg, nwd, *refs):
    moments, (wg, wu, wd), outs, (sem_out, sem_mo) = refs[:6], refs[6:9], refs[9:15], refs[15:]

    def moment(j):
        return pltpu.make_async_copy(moments[j], outs[j], sem_mo.at[j])

    def store(g, act):
        layer, i = 1 - g // NL, g % NL
        f = strips_of(i)

        @pl.loop(0, 8)
        def _(b):
            rows = pl.ds(pl.multiple_of(80 * b, 80), 80)
            for q, out in enumerate((wg, wu)):
                for k in range(2):
                    src = nwg.at[g, b % 2, b // 2, pl.ds(80 * q, 80), pl.ds(S * k, S)]
                    getattr(pltpu.make_async_copy(src, out.at[layer, rows, pl.ds(f[k], S)], sem_out.at[0]), act)()

        for core in range(2):
            for k in range(2):
                dest, off = down_piece(i, core, k)
                rows = pl.ds(pl.multiple_of(640 * dest + 320 * core + off, 64), 64)
                getattr(pltpu.make_async_copy(nwd.at[g, core, k], wd.at[layer, rows], sem_out.at[1]), act)()

    for j in range(6):
        moment(j).start()

    @pl.loop(0, NG)
    def _(g):
        store(g, "start")

    for j in range(6):
        moment(j).wait()

    @pl.loop(0, NG)
    def _(g):
        store(g, "wait")


def finish(*arrays):
    anyspace = pl.BlockSpec(memory_space=pl.ANY)
    sds = jax.ShapeDtypeStruct
    dma = pltpu.SemaphoreType.DMA
    moments = [sds(one.shape, one.dtype) for one in arrays[2:]]
    return pl.pallas_call(
        place,
        out_shape=(sds((2, D, FF), BF), sds((2, D, FF), BF), sds((2, FF, D), BF), *moments),
        in_specs=[pl.BlockSpec(memory_space=pltpu.VMEM)] * 8,
        out_specs=(anyspace,) * 9,
        scratch_shapes=[
            dma((2,)), dma((6,)),
        ],
        compiler_params=pltpu.CompilerParams(vmem_limit_bytes=2000000),
        name="place",
    )(*(pltpu.with_memory_space_constraint(one, pltpu.VMEM) for one in arrays))


def solution(mesh):
    def step(x, dy, *arrays):
        return finish(*train(x[0], dy[0], *arrays)[:8])

    whole = P(None, None, None)
    rows = P(None, "dp", None)
    seq = P(("rep", "dp"), None, None)
    return jax.shard_map(
        step,
        mesh=mesh,
        in_specs=(seq, seq) + (whole,) * 3 + (rows,) * 6,
        out_specs=(P("rep", None, None),) * 3 + (P("rep", "dp", None),) * 6,
        check_vma=False,
    )
```

time: 301 us -> 291 us (0.967)
  Pallas kernels: 300 us -> 289 us
    pallas_call x1, Pallas kernels: 287 us -> 280 us  [train(): pl.pallas_call(kernel, out_shape=outs, in_specs=[anyspace] * 11, out_spec...]
    pallas_call x1, Pallas kernels: 13.3 us -> 9.43 us  [finish(): pl.pallas_call(place, out_shape=(sds((2, D, FF), BF), sds((2, D, FF), BF)...]
where the time goes in v4:
time: 291 us; the launch traced here: 290 us
  Pallas kernels  289 us (99%)
    pallas_call x1, Pallas kernels, train(): pl.pallas_call(kernel, out_shape=outs, in_specs=[anyspace] * 11, out_spec...  280 us
    pallas_call x1, Pallas kernels, finish(): pl.pallas_call(place, out_shape=(sds((2, D, FF), BF), sds((2, D, FF), BF)...  9.43 us

profile of v4, /device:TPU:0, one launch (start us, length us, event | category | flops | bytes accessed | tf_op | source)
XLA Modules:
  0.0 290.2 jit_solution(77687531351305819)
XLA Ops:
  0.6 279.9 %train.1 = (bf16[20,2,4,160,256]{4,3,2,1,0:T(8,128)(2,1)S(1)}, bf16[20,2,2,64,640]{4,3,2,1,0:T(8,128)(2,1)S(1)}, f32[2,80,2560]{2,1,0:T(8,128)S(1)}, f32[2,80,25...) custom-call(bf16[2048,640]{1,0:T(8,128)(2,1)} %bitcast.2, ...), custom_call_target="tpu_custom_call" | custom-call | tf_op jit(solution)/shard_map/train/pallas_call | solution.py:598
  280.6 9.4 %place.1 = (bf16[2,640,2560]{2,1,0:T(8,128)(2,1)}, bf16[2,640,2560]{2,1,0:T(8,128)(2,1)}, bf16[2,2560,640]{2,1,0:T(8,128)(2,1)}, f32[2,80,2560]{2,1,0:T(8,128)},...) custom-call(bf16[20,2,4,160,256]{4,3,2,1,0:T(8,128)(2,1)S(1)} %get-t, ...), custom_call_target="tpu_custom_call" | custom-call | tf_op jit(solution)/shard_map/place/pallas_call | solution.py:662

commit v5 on v4

--- a/solution.py
+++ b/solution.py
@@ -20,17 +20,44 @@
 WS = 4
 OWN = 3
 KEEP = 4
-RING = 8
+RING = 6
 PARTS = 5
 FIRST = 2
 SCHEDULE = (
-    ("partner", "g", 0, 2), ("partner", "d", 0, 1), ("partner", "g", 1, 5), ("partner", "d", 1, 7),
-    ("sum", "g", 0, 3, 2), ("sum", "d", 0, 3, 3), ("sum", "g", 0, 2, 2), ("sum", "d", 0, 2, 1), ("sum", "g", 0, 1, 6), ("sum", "d", 0, 1, 3),
-    ("sum", "g", 1, 3, 5), ("sum", "d", 1, 3, 9), ("sum", "g", 1, 2, 6), ("sum", "d", 1, 2, 7), ("sum", "g", 2, 3, 9), ("sum", "d", 2, 3, 11),
-    ("final", "g", 1, 9), ("final", "d", 1, 11), ("final", "g", 0, 14), ("final", "d", 0, 15), ("sent", 12), ("sums_sent", 18),
-    ("gather", "g", 2, 1, 12), ("gather", "d", 2, 1, 13), ("gather", "g", 1, 0, 17), ("gather", "d", 1, 0, 17),
-    ("gather", "g", 3, 1, 19), ("gather", "d", 3, 1, 23), ("gather", "g", 2, 0, 20), ("gather", "d", 2, 0, 21),
-    ("gather", "g", 3, 0, 26), ("gather", "d", 3, 0, 25), ("gather", "g", 3, 2, 21), ("gather", "d", 3, 2, 17),
+    ("partner", "g", 0, 1),
+    ("partner", "g", 1, 4),
+    ("partner", "d", 0, 1),
+    ("partner", "d", 1, 6),
+    ("sum", "g", 0, 3, 1),
+    ("sum", "d", 0, 3, 2),
+    ("sum", "g", 0, 2, 1),
+    ("sum", "d", 0, 2, 1),
+    ("sum", "g", 0, 1, 5),
+    ("sum", "d", 0, 1, 3),
+    ("sum", "g", 1, 3, 4),
+    ("sum", "d", 1, 3, 7),
+    ("sum", "g", 1, 2, 5),
+    ("sum", "d", 1, 2, 6),
+    ("sum", "g", 2, 3, 7),
+    ("sum", "d", 2, 3, 9),
+    ("final", "g", 1, 8),
+    ("final", "d", 1, 9),
+    ("final", "g", 0, 13),
+    ("final", "d", 0, 14),
+    ("gather", "g", 2, 1, 11),
+    ("gather", "d", 2, 1, 12),
+    ("gather", "g", 1, 0, 17),
+    ("gather", "d", 1, 0, 18),
+    ("gather", "g", 3, 1, 13),
+    ("gather", "d", 3, 1, 23),
+    ("gather", "g", 2, 0, 20),
+    ("gather", "d", 2, 0, 20),
+    ("gather", "g", 3, 0, 25),
+    ("gather", "d", 3, 0, 29),
+    ("gather", "g", 3, 2, 20),
+    ("gather", "d", 3, 2, 24),
+    ("sent", 12),
+    ("sums_sent", 18),
 )
 LAST = max((FIRST + one[-1]) // PARTS for one in SCHEDULE)
 
@@ -444,7 +471,11 @@
         each(x_again(t), "wait")
     def last_forward(t):
         rows, total = forward_tile(NL // 2 - 1, t)
-        total = (ACC[rows, :] + total).astype(BF).astype(F32)
+        ACC[rows, :] += total
+
+    def layer_input(t):
+        rows = pl.ds(t * TILE, TILE)
+        total = ACC[rows, :].astype(BF).astype(F32)
         ACC[rows, :] = jnp.zeros((TILE, D), F32)
         ha = (DGU[rows, :].astype(F32) + total[:, :512]).astype(BF)
         hb = (HID[rows, :128].astype(F32) + total[:, 512:]).astype(BF)
@@ -456,15 +487,20 @@
         A[rows, :512] = (ha * scale).astype(BF)
         A[rows, 512:] = (hb * scale).astype(BF)
         AT[:, rows] = A[rows, :].T
+        YT[:, rows] = Y[rows, :].T
+
+    y_in.wait()
+    last_forward(0)
+
+    for t in range(1, NT):
+        last_forward(t)
+        layer_input(t - 1)
+    layer_input(NT - 1)
+
+    @pl.loop(0, NT)
+    def _(t):
         each(h1_out(t), "start")
 
-    @pl.loop(0, NT // 2)
-    def _(i):
-        last_forward(2 * i)
-        last_forward(2 * i + 1)
-
-    y_in.wait()
-    turn(Y, YT)
     each(moments_in(), "wait")
     pl.semaphore_wait(barrier, 1 + jnp.where(z > 0, 1, 0) + jnp.where(z < 3, 1, 0))
 
@@ -487,11 +523,11 @@
             rows = pl.ds(t * TILE, TILE)
             ACC[rows, :] += dot_t(DGU[rows, :], WGU[slot])
 
-    def last_input_grad(g):
-        slot = (g + NL) % WS
-        for t in range(NT):
-            tile_in(h1_h, t).wait()
-        @pl.loop(0, NT)
+    def layer_change(slot, first):
+        for t in range(2):
+            tile_in(h1_h, first + t).wait()
+
+        @pl.loop(first, first + 2)
         def _(t):
             rows = tile_of(t)
             ct = (ACC[rows, :] + dot_t(DGU[rows, :], WGU[slot])).astype(BF).astype(F32)
@@ -501,7 +537,6 @@
             y = (Y[rows, :].astype(F32) + by_h.astype(BF).astype(F32)).astype(BF)
             Y[rows, :] = y
             YT[:, rows] = y.T
-        for t in range(NT):
             tile_in(a0_h, t).start()
 
     def weight_grads(g):
@@ -534,16 +569,22 @@
 
             @pl.when(g == NL)
             def _():
-                for t in range(NT):
+                layer_change((2 * NL - 1) % WS, 2)
+                for t in range(2):
                     tile_in(a0_h, t).wait()
-                turn(A, AT)
 
             keep_weights(g)
             tiles(g, 0, 2)
         elif s == 1:
+            @pl.when(g == NL)
+            def _():
+                for t in range(2, NT):
+                    tile_in(a0_h, t).wait()
+
             tiles(g, 2, 4)
             pl.when(g == NL - 1)(lambda: tiles_in(h1_h))
         elif s == 2:
+            pl.when(g == NL)(lambda: turn(A, AT))
             weight_grads(g)
             own_copies(g)[0]().start()
         elif s == 3:
@@ -551,7 +592,7 @@
             own_copies(g)[1]().start()
         else:
             pl.when(g < NL - 1)(lambda: input_grad(g))
-            pl.when(g == NL - 1)(lambda: last_input_grad(g))
+            pl.when(g == NL - 1)(lambda: layer_change((2 * NL - 1) % WS, 0))
 
     @pl.loop(0, NG + LAST)
     def _(g):
@@ -610,7 +651,7 @@
             dma((NG, 5)), dma((NG, 2, 2)), dma((NG, 4)), dma((NG, 2)), dma((2,)),
         ],
         compiler_params=pltpu.CompilerParams(
-            collective_id=0, has_side_effects=True, vmem_limit_bytes=37000000),
+            collective_id=0, has_side_effects=True, vmem_limit_bytes=37500000),
         name="train",
     )(x, dy, *arrays)
 

time: 291 us -> 286 us (0.983)
  Pallas kernels: 289 us -> 285 us
    pallas_call x1, Pallas kernels: 280 us -> 276 us  [train(): pl.pallas_call(kernel, out_shape=outs, in_specs=[anyspace] * 11, out_spec...]
where the time goes in v5:
time: 286 us
  Pallas kernels  285 us (100%)
    pallas_call x1, Pallas kernels, train(): pl.pallas_call(kernel, out_shape=outs, in_specs=[anyspace] * 11, out_spec...  276 us
    pallas_call x1, Pallas kernels, finish(): pl.pallas_call(place, out_shape=(sds((2, D, FF), BF), sds((2, D, FF), BF)...  9.43 us

profile of v5, /device:TPU:0, one launch (start us, length us, event | category | flops | bytes accessed | tf_op | source)
XLA Modules:
  0.0 285.9 jit_solution(5371297217249361884)
XLA Ops:
  0.6 275.7 %train.1 = (bf16[20,2,4,160,256]{4,3,2,1,0:T(8,128)(2,1)S(1)}, bf16[20,2,2,64,640]{4,3,2,1,0:T(8,128)(2,1)S(1)}, f32[2,80,2560]{2,1,0:T(8,128)S(1)}, f32[2,80,25...) custom-call(bf16[2048,640]{1,0:T(8,128)(2,1)} %bitcast.2, ...), custom_call_target="tpu_custom_call" | custom-call | tf_op jit(solution)/shard_map/train/pallas_call | solution.py:639
  276.3 9.4 %place.1 = (bf16[2,640,2560]{2,1,0:T(8,128)(2,1)}, bf16[2,640,2560]{2,1,0:T(8,128)(2,1)}, bf16[2,2560,640]{2,1,0:T(8,128)(2,1)}, f32[2,80,2560]{2,1,0:T(8,128)},...) custom-call(bf16[20,2,4,160,256]{4,3,2,1,0:T(8,128)(2,1)S(1)} %get-t, ...), custom_call_target="tpu_custom_call" | custom-call | tf_op jit(solution)/shard_map/place/pallas_call | solution.py:703

commit v6 on v5

--- a/solution.py
+++ b/solution.py
@@ -23,42 +23,26 @@
 RING = 6
 PARTS = 5
 FIRST = 2
-SCHEDULE = (
-    ("partner", "g", 0, 1),
-    ("partner", "g", 1, 4),
-    ("partner", "d", 0, 1),
-    ("partner", "d", 1, 6),
-    ("sum", "g", 0, 3, 1),
-    ("sum", "d", 0, 3, 2),
-    ("sum", "g", 0, 2, 1),
-    ("sum", "d", 0, 2, 1),
-    ("sum", "g", 0, 1, 5),
-    ("sum", "d", 0, 1, 3),
-    ("sum", "g", 1, 3, 4),
-    ("sum", "d", 1, 3, 7),
-    ("sum", "g", 1, 2, 5),
-    ("sum", "d", 1, 2, 6),
-    ("sum", "g", 2, 3, 7),
-    ("sum", "d", 2, 3, 9),
-    ("final", "g", 1, 8),
-    ("final", "d", 1, 9),
-    ("final", "g", 0, 13),
-    ("final", "d", 0, 14),
-    ("gather", "g", 2, 1, 11),
-    ("gather", "d", 2, 1, 12),
-    ("gather", "g", 1, 0, 17),
-    ("gather", "d", 1, 0, 18),
-    ("gather", "g", 3, 1, 13),
-    ("gather", "d", 3, 1, 23),
-    ("gather", "g", 2, 0, 20),
-    ("gather", "d", 2, 0, 20),
-    ("gather", "g", 3, 0, 25),
-    ("gather", "d", 3, 0, 29),
-    ("gather", "g", 3, 2, 20),
-    ("gather", "d", 3, 2, 24),
-    ("sent", 12),
-    ("sums_sent", 18),
+TIMES = (
+    ("partner", (0,), 1, 1),
+    ("partner", (1,), 4, 6),
+    ("sum", (0, 3,), 1, 2),
+    ("sum", (0, 2,), 1, 1),
+    ("sum", (0, 1,), 5, 3),
+    ("sum", (1, 3,), 4, 7),
+    ("sum", (1, 2,), 5, 6),
+    ("sum", (2, 3,), 7, 9),
+    ("final", (1,), 8, 9),
+    ("final", (0,), 13, 14),
+    ("gather", (2, 1,), 11, 12),
+    ("gather", (1, 0,), 17, 18),
+    ("gather", (3, 1,), 13, 23),
+    ("gather", (2, 0,), 20, 20),
+    ("gather", (3, 0,), 25, 29),
+    ("gather", (3, 2,), 20, 24),
 )
+SCHEDULE = [(step, kind, *chips, when) for step, chips, *both in TIMES for kind, when in zip("gd", both)]
+SCHEDULE += [("sent", 12), ("sums_sent", 18)]
 LAST = max((FIRST + one[-1]) // PARTS for one in SCHEDULE)
 
 
@@ -120,8 +104,11 @@
     def to(dz, flip=False):
         return (rep, (z + dz) * 2 + ((1 - c) if flip else c))
 
+    def other_core():
+        return to(0, True)
+
     barrier = pltpu.get_barrier_semaphore()
-    pl.semaphore_signal(barrier, inc=1, device_id=to(0, True), device_id_type=MESH)
+    pl.semaphore_signal(barrier, inc=1, device_id=other_core(), device_id_type=MESH)
 
     @pl.when(z > 0)
     def _():
@@ -190,10 +177,10 @@
             remote(p_d.at[g % RING, k], nwd.at[g, c, k], sem_rs.at[g % RING, 4 + k], sem_rd.at[g, k, side], to(dz)).start()
 
     def wait_rg(g, slot):
-        remote(p_g.at[g % RING, 0], x_g.at[g % RING], sem_send.at[0], sem_rg.at[g, slot], to(0, True)).wait_recv()
+        remote(p_g.at[g % RING, 0], x_g.at[g % RING], sem_send.at[0], sem_rg.at[g, slot], other_core()).wait_recv()
 
     def wait_rd(g, k, side):
-        remote(p_d.at[g % RING, k], x_d.at[g // 2 % (RING // 2), k], sem_send.at[1], sem_rd.at[g, k, side], to(0, True)).wait_recv()
+        remote(p_d.at[g % RING, k], x_d.at[g // 2 % (RING // 2), k], sem_send.at[1], sem_rd.at[g, k, side], other_core()).wait_recv()
 
     def ag_start_g(g, d, dz):
         here = nwg.at[g, c, d]
@@ -205,27 +192,27 @@
 
     def partner_start_g(g, d):
         here = nwg.at[g, c, d]
-        remote(here, here, sem_send.at[6], sem_pa.at[0], to(0, True)).start()
+        remote(here, here, sem_send.at[6], sem_pa.at[0], other_core()).start()
 
     def partner_start_d(g, k):
         here = nwd.at[g, c, k]
-        remote(here, here, sem_send.at[7], sem_pa.at[1], to(0, True)).start()
+        remote(here, here, sem_send.at[7], sem_pa.at[1], other_core()).start()
 
     def wait_ag(g, d):
         here = nwg.at[g, c, d]
-        remote(here, here, sem_send.at[2], sem_ag.at[g, d], to(0, True)).wait_recv()
+        remote(here, here, sem_send.at[2], sem_ag.at[g, d], other_core()).wait_recv()
 
     def wait_ad(g, k):
         here = nwd.at[g, c, k]
-        remote(here, here, sem_send.at[4], sem_ad.at[g, k], to(0, True)).wait_recv()
+        remote(here, here, sem_send.at[4], sem_ad.at[g, k], other_core()).wait_recv()
 
     def own_copies(g):
         slot = g % OWN
         return (
             functools.partial(pltpu.make_async_remote_copy,
-                own_g.at[slot, 1 - c], p_g.at[g % RING], sem_own.at[slot, 0], sem_pg.at[g], device_id=to(0, True), device_id_type=MESH),
+                own_g.at[slot, 1 - c], p_g.at[g % RING], sem_own.at[slot, 0], sem_pg.at[g], device_id=other_core(), device_id_type=MESH),
             functools.partial(pltpu.make_async_remote_copy,
-                own_d.at[slot, 1 - c], p_d.at[g % RING], sem_own.at[slot, 1], sem_pd.at[g], device_id=to(0, True), device_id_type=MESH),
+                own_d.at[slot, 1 - c], p_d.at[g % RING], sem_own.at[slot, 1], sem_pd.at[g], device_id=other_core(), device_id_type=MESH),
         )
 
     def sum_of(*terms):
@@ -364,7 +351,7 @@
         slot = g % RING
 
         def wait(ref, at):
-            remote(ref, ref, sem_rs.at[slot, at], sem_pa.at[0], to(0, True)).wait_send()
+            remote(ref, ref, sem_rs.at[slot, at], sem_pa.at[0], other_core()).wait_send()
 
         for j in range(4):
             pl.when(z != j)(lambda j=j: wait(p_g.at[slot, j], j))
@@ -420,8 +407,8 @@
         tile_in(x_h, t).start()
     a_out = pltpu.make_async_copy(A, a0_h, sem_in.at[NT])
 
-    def forward_tile(n, t):
-        rows = pl.ds(t * TILE, TILE) if isinstance(t, int) else tile_of(t)
+    def forward_tile(n, t, size=TILE):
+        rows = pl.ds(t * size, size)
         a = A[rows, :]
         total = 0.0
         for slot in ((2 * n) % WS, (2 * n + 1) % WS):
@@ -454,15 +441,19 @@
         ACC[rows, :] = total
     a_out.start()
     y_in.start()
-    for t in range(NT):
-        each(x_again(t), "start")
-    each(moments_in(), "start")
 
     @pl.loop(1, NL // 2 - 1)
     def _(n):
         forward_weights(n)
-        for t in range(NT):
-            rows, total = forward_tile(n, t)
+
+        @pl.when(n == 2)
+        def _():
+            for t in range(NT):
+                each(x_again(t), "start")
+
+        pl.when(n == 3)(lambda: each(moments_in(), "start"))
+        for t in range(NT // 2):
+            rows, total = forward_tile(n, t, 2 * TILE)
             ACC[rows, :] += total
 
     a_out.wait()
@@ -601,7 +592,7 @@
             tick(g, s)
 
     def all_of(ref, send, recv):
-        return remote(ref, ref, send, recv, to(0, True))
+        return remote(ref, ref, send, recv, other_core())
 
     all_of(nwg.at[:, 1 - c], sem_send.at[6], sem_pa.at[0]).wait_recv()
     all_of(nwd.at[:, 1 - c], sem_send.at[7], sem_pa.at[1]).wait_recv()

time: 286 us -> 286 us (level)
  no operation moved by 1% of the time
where the time goes in v6:
time: 286 us
  Pallas kernels  285 us (100%)
    pallas_call x1, Pallas kernels, train(): pl.pallas_call(kernel, out_shape=outs, in_specs=[anyspace] * 11, out_spec...  276 us
    pallas_call x1, Pallas kernels, finish(): pl.pallas_call(place, out_shape=(sds((2, D, FF), BF), sds((2, D, FF), BF)...  9.43 us

profile of v6, /device:TPU:0, one launch (start us, length us, event | category | flops | bytes accessed | tf_op | source)
XLA Modules:
  0.0 285.9 jit_solution(5057216256954847316)
XLA Ops:
  0.6 275.6 %train.1 = (bf16[20,2,4,160,256]{4,3,2,1,0:T(8,128)(2,1)S(1)}, bf16[20,2,2,64,640]{4,3,2,1,0:T(8,128)(2,1)S(1)}, f32[2,80,2560]{2,1,0:T(8,128)S(1)}, f32[2,80,25...) custom-call(bf16[2048,640]{1,0:T(8,128)(2,1)} %bitcast.2, ...), custom_call_target="tpu_custom_call" | custom-call | tf_op jit(solution)/shard_map/train/pallas_call | solution.py:630
  276.3 9.4 %place.1 = (bf16[2,640,2560]{2,1,0:T(8,128)(2,1)}, bf16[2,640,2560]{2,1,0:T(8,128)(2,1)}, bf16[2,2560,640]{2,1,0:T(8,128)(2,1)}, f32[2,80,2560]{2,1,0:T(8,128)},...) custom-call(bf16[20,2,4,160,256]{4,3,2,1,0:T(8,128)(2,1)S(1)} %get-t, ...), custom_call_target="tpu_custom_call" | custom-call | tf_op jit(solution)/shard_map/place/pallas_call | solution.py:694
